TPU v7x, 32 devices: a whole 2x2x4 slice. The times are simulated.
32 devices in a mesh: tm: 16 (over z, y, x), head: 2 (over core).
Axes of the slice: x: 2, y: 2, z: 4, core: 2. Of those that a mesh axis runs over, the one named last changes fastest.
Arguments:
- queries: bfloat16 [2048, 6144], P('tm', 'head'), may hold values from -150 to 150
- window_keys: bfloat16 [2048, 6144], P('tm', 'head'), may hold values from -6 to 6
- window_values: bfloat16 [2048, 6144], P('tm', 'head'), may hold values from -6 to 6
- context_keys: bfloat16 [2048, 6144], P('tm', 'head'), may hold values from -6 to 6
- context_values: bfloat16 [2048, 6144], P('tm', 'head'), may hold values from -6 to 6
- block_group: int32 [64], replicated, may hold values from 0 to 15, never falling along the last dimension, each value on 1 to 8 neighbouring positions
- sees: int32 [16, 16], replicated, may hold values from 0 to 1, as said below
- out_weight: bfloat16 [6144, 6144], P('head'), may hold values from -1 to 1
- gate: float32 [6144], P('head'), may hold values from 0.5 to 2
Outputs:
- update: bfloat16 [2048, 6144], P('tm', 'head')
Inputs may be any that keep to these rules, and one draw needn't show every extreme that they name: sees[a, a] is 1 and sees[a, b] is 0 for b > a. `block_group`: never falling along the blocks.
All inputs are finite; a program needn't handle non-finite values.
Results may differ from a plain program's by a relative error of at most 0.03.
Values may be sent and summed in bfloat16 or wider, within the bound.
No kernel may reach another device: no remote copies, remote signals or barrier semaphores. Data moves between devices by JAX's collectives and lax.ppermute only.
A program may use at most 192 MiB of HBM per device.

v0:
```python
import jax
import jax.numpy as jnp
from jax import lax
from jax.sharding import PartitionSpec as P

HD = 128
BLOCK = 64


def group_rows(positions, group_table, group_count):
    blocks = positions // BLOCK
    picker = (blocks[:, None] == jnp.arange(group_table.shape[0], dtype=jnp.int32)[None, :]).astype(
        jnp.float32
    )
    group_ids = jnp.dot(picker, group_table, precision=lax.Precision.HIGHEST)
    return (group_ids[:, None] == jnp.arange(group_count, dtype=jnp.float32)[None, :]).astype(
        jnp.float32
    )


def body(
    queries,
    window_keys,
    window_values,
    context_keys,
    context_values,
    block_group,
    sees,
    out_weight,
    gate,
):
    tok_rows = queries.shape[0]
    features = queries.shape[1]
    local_heads = features // HD
    tm_count = lax.axis_size("tm")
    own_index = lax.axis_index("tm")
    ctx_rows = context_keys.shape[0]
    ctx_total = ctx_rows * tm_count
    group_count = sees.shape[0]
    group_table = block_group.astype(jnp.float32)
    sees_table = sees.astype(jnp.float32)
    score_scale = 1.0 / jnp.sqrt(jnp.float32(HD))
    all_queries = lax.all_gather(queries, "tm", axis=0, tiled=True)
    win_rows = all_queries.shape[0]
    query_pos = ctx_total + jnp.arange(win_rows, dtype=jnp.int32)
    key_pos = jnp.concatenate(
        [
            own_index * ctx_rows + jnp.arange(ctx_rows, dtype=jnp.int32),
            ctx_total + own_index * tok_rows + jnp.arange(tok_rows, dtype=jnp.int32),
        ]
    )
    query_sees = jnp.dot(
        group_rows(query_pos, group_table, group_count), sees_table, precision=lax.Precision.HIGHEST
    )
    key_onehot = group_rows(key_pos, group_table, group_count)
    visible = jnp.dot(query_sees, key_onehot.T, precision=lax.Precision.HIGHEST) > 0.5
    key_piece = jnp.concatenate([context_keys, window_keys], axis=0).reshape(
        ctx_rows + tok_rows, local_heads, HD
    )
    value_piece = jnp.concatenate([context_values, window_values], axis=0).reshape(
        ctx_rows + tok_rows, local_heads, HD
    )
    query_heads = all_queries.reshape(win_rows, local_heads, HD)
    scores = (
        jnp.einsum("qhd,khd->hqk", query_heads, key_piece, preferred_element_type=jnp.float32)
        * score_scale
    )
    scores = jnp.where(visible[None], scores, jnp.float32(-1e30))
    row_peak = lax.pmax(jnp.max(scores, axis=-1).astype(jnp.bfloat16), "tm").astype(jnp.float32)
    weights = jnp.where(visible[None], jnp.exp(scores - row_peak[..., None]), jnp.float32(0.0))
    totals = jnp.sum(weights, axis=-1).T
    numer = jnp.einsum(
        "hqk,khd->qhd",
        weights.astype(jnp.bfloat16),
        value_piece,
        preferred_element_type=jnp.float32,
    ).reshape(win_rows, features)
    numer_mine, totals_mine = (
        lax.psum_scatter(numer.astype(jnp.bfloat16), "tm", scatter_dimension=0, tiled=True).astype(
            jnp.float32
        ),
        lax.psum_scatter(totals.astype(jnp.bfloat16), "tm", scatter_dimension=0, tiled=True).astype(
            jnp.float32
        ),
    )
    attended = (
        (numer_mine.reshape(tok_rows, local_heads, HD) / totals_mine[..., None])
        .reshape(tok_rows, features)
        .astype(jnp.bfloat16)
    )
    projected = jnp.dot(attended, out_weight, preferred_element_type=jnp.float32)
    summed = lax.psum_scatter(
        projected.astype(jnp.bfloat16), "head", scatter_dimension=1, tiled=True
    ).astype(jnp.float32)
    return (gate[None, :] * summed).astype(jnp.bfloat16)


def solution(mesh):
    placed = (
        P("tm", "head"),
        P("tm", "head"),
        P("tm", "head"),
        P("tm", "head"),
        P("tm", "head"),
        P(),
        P(),
        P("head", None),
        P("head"),
    )
    return jax.shard_map(
        body, mesh=mesh, in_specs=placed, out_specs=P("tm", "head"), check_vma=False
    )
```

profile of v0, /device:TPU:0, one launch (start us, length us, event | category | flops | bytes accessed | tf_op | source)
XLA Modules:
  0.0 677.0 jit_solution(15997595221574299560)
XLA Ops:
  6.5 0.0 all-gather.2.cloned.1.call-start
  6.5 2.3 copy.25
  8.8 0.0 all-gather.2.cloned.1.call-update
  8.9 0.0 all-reduce.2.cloned.1.call-start
  9.0 0.8 fusion.18
  9.8 1.4 fusion.15
  11.2 1.5 fusion.14
  12.7 1.2 convolution_compare_fusion
  13.9 1.0 copy.22
  14.9 1.5 copy.23
  16.4 2.3 copy.24
  18.7 1.3 pad_maximum_fusion.1
  20.0 188.2 %all-gather.2.cloned.1.call-done = bf16[2048,3072]{0,1:T(8,128)(2,1)} async-done(((bf16[128,3072]{0,1:T(8,128)(2,1)}), bf16[2048,3072]{0,1:T(8,128)(2,1)}) %all-gather.2.cloned.1.call-update) | async-done | bytes 12582928 | tf_op jit(solution)/shard_map/all_gather | solution.py:43
  208.2 0.0 copy-start.1
  208.2 24.9 %fusion = (bf16[24,2048]{1,0:T(8,128)(2,1)}, f32[24,256,2048]{2,1,0:T(8,128)}) fusion(pred[2048,256]{0,1:T(8,128)(4,1)S(1)} %copy.22, bf16[256,24,128]{0,2,1:T(8,128)(2,1)S(1)} %bitcast.44, bf16[2048,24,128]{0,2,1:T(8,128)(2,1)} %bitcast.42), kind=kOutput, calls=%fused_computation.2 | convolution fusion | flops 3258925056 | bytes 65110016 | tf_op jit(solution)/shard_map/qhd,khd->hqk/dot_general | solution.py:65
  233.2 0.0 all-reduce.2.cloned.1.call-update
  233.2 0.0 reduce-scatter.12.cloned.1.call-start
  233.3 0.0 copy-done.1
  233.3 1.2 pad_maximum_fusion
  234.5 1.6 copy.21
  236.1 100.0 %all-reduce.2.cloned.1.call-done = bf16[24,2048]{1,0:T(8,128)(2,1)} async-done(((bf16[24,2048]{1,0:T(8,128)(2,1)}), bf16[24,2048]{1,0:T(8,128)(2,1)}) %all-reduce.2.cloned.1.call-update) | async-done | bytes 98320 | tf_op jit(solution)/shard_map/pmax | solution.py:69
  336.1 0.9 convert_element_type.55
  337.0 0.0 copy-start
  337.1 21.7 %fusion.1 = bf16[24,2048]{1,0:T(8,128)(2,1)S(1)} fusion(f32[24,256,2048]{2,1,0:T(8,128)} %get-tuple-element.6, f32[24,2048]{1,0:T(8,128)S(1)} %convert_element_type.55, pred[2048,256]{0,1:T(8,128)(4,1)S(1)} %copy.22), kind=kLoop, calls=%fused_computation.3 | loop fusion | flops 62865408 | bytes 51150848 | tf_op jit(solution)/shard_map/reduce_sum | solution.py:71
  358.8 1.0 copy.34
  359.8 0.0 reduce-scatter.12.cloned.1.call-update
  359.8 0.2 reduce-scatter.10.cloned.1.call-start
  360.0 0.0 copy-done
  360.0 24.3 %fusion.10 = bf16[24,128,2048]{2,1,0:T(8,128)(2,1)} fusion(bf16[256,24,128]{0,2,1:T(8,128)(2,1)S(1)} %bitcast.45, f32[24,256,2048]{2,1,0:T(8,128)} %get-tuple-element.6, f32[24,2048]{1,0:T(8,128)S(1)} %convert_element_type.55, pred[2048,256]{0,1:T(8,128)(4,1)S(1)} %copy.22), kind=kOutput, calls=%fused_computation.12 | convolution fusion | flops 3290431488 | bytes 65208320 | tf_op jit(solution)/shard_map/hqk,khd->qhd/dot_general | solution.py:72
  384.3 16.6 %copy.32 = bf16[2048,3072]{1,0:T(8,128)(2,1)} copy(bf16[2048,3072]{0,1:T(8,128)(2,1)} %bitcast.43) | data formatting | bytes 25165824
  400.9 0.0 reduce-scatter.10.cloned.1.call-update
  400.9 0.0 reduce-scatter.8.cloned.1.call-start
  401.0 36.4 %reduce-scatter.12.cloned.1.call-done = bf16[128,24]{1,0:T(8,128)(2,1)} async-done(((bf16[2048,24]{1,0:T(8,128)(2,1)}), bf16[128,24]{1,0:T(8,128)(2,1)}) %reduce-scatter.12.cloned.1.call-update) | async-done | bytes 6160
  437.4 0.8 copy.35
  438.3 203.8 %reduce-scatter.10.cloned.1.call-done = bf16[128,3072]{1,0:T(8,128)(2,1)} async-done(((bf16[2048,3072]{1,0:T(8,128)(2,1)}), bf16[128,3072]{1,0:T(8,128)(2,1)}) %reduce-scatter.10.cloned.1.call-update) | async-done | bytes 786448
  642.0 1.5 copy.33
  643.5 0.2 fusion.13
  643.7 0.0 copy-start.2
  643.7 15.9 %convolution_convert_fusion = bf16[128,6144]{1,0:T(8,128)(2,1)} fusion(bf16[128,3072]{0,1:T(8,128)(2,1)S(1)} %fusion.13, bf16[3072,6144]{1,0:T(8,128)(2,1)} %param.16), kind=kOutput, calls=%fused_computation.11 | convolution fusion | flops 4832624640 | bytes 40108032 | tf_op jit(solution)/shard_map/dot_general | solution.py:91
  659.6 0.0 reduce-scatter.8.cloned.1.call-update
  659.6 8.6 %reduce-scatter.8.cloned.1.call-done = bf16[128,3072]{1,0:T(8,128)(2,1)} async-done(((bf16[128,6144]{1,0:T(8,128)(2,1)}), bf16[128,3072]{1,0:T(8,128)(2,1)}) %reduce-scatter.8.cloned.1.call-update) | async-done | bytes 786448 | tf_op jit(solution)/shard_map/reduce_scatter | solution.py:92
  668.3 0.0 copy-done.2
  668.3 2.2 multiply_convert_fusion
  (4 shorter events, 0.0 us)
Async XLA Ops:
  6.5 201.7 %all-gather.2.cloned.1.call-start = ((), (), s32[]{:S(2)}) async-start(), calls=%async_computation.3 | async-start | bytes 13369344 | tf_op jit(solution)/shard_map/all_gather | solution.py:43
  8.9 327.3 %all-reduce.2.cloned.1.call-start = ((), (), s32[]{:S(2)}) async-start(), calls=%async_computation.4 | async-start | bytes 196608 | tf_op jit(solution)/shard_map/pmax | solution.py:69
  208.2 25.0 %copy-start.1 = (bf16[128,3072]{1,0:T(8,128)(2,1)S(1)}, bf16[128,3072]{1,0:T(8,128)(2,1)}, u32[]{:S(2)}) copy-start(bf16[128,3072]{1,0:T(8,128)(2,1)} %param.11) | copy-start | bytes 2359300
  233.2 204.2 %reduce-scatter.12.cloned.1.call-start = ((), (), s32[]{:S(2)}) async-start(), calls=%async_computation.7 | async-start | bytes 557056
  337.0 23.0 %copy-start = (bf16[256,3072]{0,1:T(8,128)(2,1)S(1)}, bf16[256,3072]{0,1:T(8,128)(2,1)}, u32[]{:S(2)}) copy-start(bf16[256,3072]{0,1:T(8,128)(2,1)} %copy.21) | copy-start | bytes 4718596
  359.8 282.2 %reduce-scatter.10.cloned.1.call-start = ((), (), s32[]{:S(2)}) async-start(), calls=%async_computation.6 | async-start | bytes 13369344
  400.9 267.3 %reduce-scatter.8.cloned.1.call-start = ((), (), s32[]{:S(2)}) async-start(), calls=%async_computation.5 | async-start | bytes 2359296 | tf_op jit(solution)/shard_map/reduce_scatter | solution.py:92
  643.7 24.6 %copy-start.2 = (f32[3072]{0:T(1024)S(1)}, f32[3072]{0:T(1024)}, u32[]{:S(2)}) copy-start(f32[3072]{0:T(1024)} %param.17) | copy-start | bytes 36868
Sparse Core Ops, SparseCore 0:
  10.0 198.1 all-gather.1
  233.3 102.7 all-reduce.1
  359.9 77.4 reduce-scatter.11
  443.0 199.0 reduce-scatter.9
  659.8 8.4 reduce-scatter.7
where the time goes:
time: 678 us; the launch traced here: 677 us
  waiting for transfers between devices  537 us (79%)
  matrix products  70 us (10%)
  local copies, waits for them, and re-layouts  28.7 us (4%)
  other arithmetic  27.5 us (4%)
  between operations  13.3 us (2%)
    unnamed x7, waiting for transfers between devices  240 us
    all_gather x1, waiting for transfers between devices, body(): all_queries = lax.all_gather(queries, 'tm', axis=0, tiled=True)  188 us
    pmax x1, waiting for transfers between devices, body(): lax.pmax(jnp.max(scores, axis=-1).astype(jnp.bfloat16), 'tm')  100 us
    unnamed x13, local copies, waits for them, and re-layouts  26 us
    dot_general x1, matrix products, body(): jnp.einsum('qhd,khd->hqk', query_heads, key_piece, preferred_element_type...  24.9 us
    dot_general x1, matrix products, body(): jnp.einsum('hqk,khd->qhd', weights.astype(jnp.bfloat16), value_piece, pre...  24.3 us
    reduce_sum x1, other arithmetic, body(): totals = jnp.sum(weights, axis=-1).T  21.7 us
    dot_general x1, matrix products, body(): jnp.dot(attended, out_weight, preferred_element_type=jnp.float32)  15.9 us
  transfers between devices with their start and end apart: 5, of which 5 were waited for; matrix products, arithmetic and copies ran while one was open for 8% of the time, Pallas kernels for 0%

commit v1 on v0

--- a/solution.py
+++ b/solution.py
@@ -1,10 +1,17 @@
+import functools
+import math
+
 import jax
 import jax.numpy as jnp
 from jax import lax
+from jax.experimental import pallas as pl
+from jax.experimental.pallas import tpu as pltpu
 from jax.sharding import PartitionSpec as P
 
 HD = 128
 BLOCK = 64
+MASKED = -1e30
+VMEM_LIMIT = 48 * 1024 * 1024
 
 
 def group_rows(positions, group_table, group_count):
@@ -18,7 +25,7 @@
     )
 
 
-def body(
+def gathered_body(
     queries,
     window_keys,
     window_values,
@@ -95,6 +102,264 @@
     return (gate[None, :] * summed).astype(jnp.bfloat16)
 
 
+def pack_kernel(q_ref, ck_ref, wk_ref, cv_ref, wv_ref, shared_ref, own_ref):
+    at_shared, at_own = 0, 0
+    for ref in (q_ref, ck_ref, wk_ref, cv_ref, wv_ref):
+        rows = ref.shape[0]
+        half = rows // 2
+        for side in range(2):
+            shared_ref[side, at_shared : at_shared + half, :] = ref[
+                side * half : (side + 1) * half, HD : 2 * HD
+            ]
+            own_ref[side, at_own : at_own + rows, :] = ref[:, 2 * side * HD : (2 * side + 1) * HD]
+        at_shared += half
+        at_own += rows
+
+
+def pack(q, ck, wk, cv, wv):
+    pairs = q.shape[1] // (3 * HD)
+    rows = [x.shape[0] for x in (q, ck, wk, cv, wv)]
+    total = sum(rows)
+    return pl.pallas_call(
+        pack_kernel,
+        grid=(pairs,),
+        in_specs=[pl.BlockSpec((r, 3 * HD), lambda j: (0, j)) for r in rows],
+        out_specs=[
+            pl.BlockSpec((2, total // 2, HD), lambda j: (j, 0, 0)),
+            pl.BlockSpec((2, total, HD), lambda j: (j, 0, 0)),
+        ],
+        out_shape=[
+            jax.ShapeDtypeStruct((2 * pairs, total // 2, HD), q.dtype),
+            jax.ShapeDtypeStruct((2 * pairs, total, HD), q.dtype),
+        ],
+        name="pack",
+    )(q, ck, wk, cv, wv)
+
+
+def attend_kernel(q_from, q_rows, sources, scale, *refs):
+    n = len(sources)
+    operands, bias_ref, out_ref, k_all, v_all = (
+        refs[:n],
+        refs[n],
+        refs[n + 1],
+        refs[n + 2],
+        refs[n + 3],
+    )
+    step = pl.program_id(0)
+
+    @pl.when(step == 0)
+    def _():
+        at = 0
+        for ref, (k_lo, k_hi, v_lo, v_hi) in zip(operands, sources):
+            count = ref.shape[0] * (k_hi - k_lo)
+            k_all[at : at + count, :] = ref[:, k_lo:k_hi, :].reshape(count, HD)
+            v_all[at : at + count, :] = ref[:, v_lo:v_hi, :].reshape(count, HD)
+            at += count
+
+    chips = out_ref.shape[0]
+    tile = chips * q_rows
+    runs = bias_ref.shape[1]
+    keys = k_all.shape[0]
+    q = operands[0][pl.ds(step * chips, chips), q_from : q_from + q_rows, :].reshape(tile, HD)
+    scores = lax.dot_general(
+        q, k_all[...], (((1,), (1,)), ((), ())), preferred_element_type=jnp.float32
+    )
+    scores = scores.reshape(runs, tile // runs, keys) * scale + bias_ref[0][:, None, :]
+    peak = jnp.max(scores, axis=-1, keepdims=True)
+    weights = jnp.exp2(scores - peak)
+    total = jnp.sum(weights, axis=-1, keepdims=True).reshape(tile, 1)
+    numer = jnp.dot(
+        weights.astype(jnp.bfloat16).reshape(tile, keys),
+        v_all[...],
+        preferred_element_type=jnp.float32,
+    )
+    out_ref[...] = (numer / total).astype(out_ref.dtype).reshape(out_ref.shape)
+
+
+def attend(operands, sources, bias, q_from, q_rows, tile_rows, name):
+    count = operands[0].shape[0]
+    chips = tile_rows // q_rows
+    keys = bias.shape[1]
+    runs = tile_rows // BLOCK
+    bias = bias.reshape(bias.shape[0] // runs, runs, keys)
+    scale = math.log2(math.e) / math.sqrt(HD)
+    work = count * q_rows * keys
+    return pl.pallas_call(
+        functools.partial(attend_kernel, q_from, q_rows, sources, scale),
+        grid=(count // chips,),
+        in_specs=[pl.BlockSpec(x.shape, lambda i: (0, 0, 0)) for x in operands]
+        + [pl.BlockSpec((1, runs, keys), lambda i: (i, 0, 0))],
+        out_specs=pl.BlockSpec((chips, q_rows, HD), lambda i: (i, 0, 0)),
+        out_shape=jax.ShapeDtypeStruct((count, q_rows, HD), jnp.bfloat16),
+        scratch_shapes=[pltpu.VMEM((keys, HD), jnp.bfloat16), pltpu.VMEM((keys, HD), jnp.bfloat16)],
+        cost_estimate=pl.CostEstimate(
+            flops=8 * work * HD, bytes_accessed=4 * 1024 * 1024, transcendentals=work
+        ),
+        compiler_params=pltpu.CompilerParams(vmem_limit_bytes=VMEM_LIMIT),
+        name=name,
+    )(*operands, bias)
+
+
+def project_kernel(which_ref, shared_ref, own_lo_ref, own_hi_ref, w_ref, out_ref, acc_ref):
+    step = pl.program_id(0)
+    rows = shared_ref.shape[0] * shared_ref.shape[1]
+
+    @pl.when(step == 0)
+    def _():
+        acc_ref[...] = jnp.zeros_like(acc_ref)
+
+    left = jnp.concatenate([own_lo_ref[0], own_hi_ref[0]], axis=0)
+    middle = shared_ref[...].reshape(rows, HD)
+    right = jnp.concatenate([own_lo_ref[1], own_hi_ref[1]], axis=0)
+    attended = jnp.concatenate([left, middle, right], axis=1)
+    acc_ref[...] += jnp.dot(attended, w_ref[...], preferred_element_type=jnp.float32)
+
+    @pl.when(step == pl.num_programs(0) - 1)
+    def _():
+        out_ref[...] = acc_ref[...].astype(out_ref.dtype)
+
+
+def project(shared, own_lo, own_hi, weight, which, columns, dtype, name):
+    pairs = shared.shape[0] // 2
+    half = shared.shape[1]
+    part = pl.BlockSpec((2, half, HD), lambda j, which: (j, 0, 0))
+    return pl.pallas_call(
+        project_kernel,
+        grid_spec=pltpu.PrefetchScalarGridSpec(
+            num_scalar_prefetch=1,
+            grid=(pairs,),
+            in_specs=[
+                part,
+                part,
+                part,
+                pl.BlockSpec((3 * HD, columns), lambda j, which: (j, which[0])),
+            ],
+            out_specs=pl.BlockSpec((2 * half, columns), lambda j, which: (0, 0)),
+            scratch_shapes=[pltpu.VMEM((2 * half, columns), jnp.float32)],
+        ),
+        out_shape=jax.ShapeDtypeStruct((2 * half, columns), dtype),
+        cost_estimate=pl.CostEstimate(
+            flops=4 * half * weight.shape[0] * columns,
+            bytes_accessed=2 * weight.shape[0] * columns,
+            transcendentals=0,
+        ),
+        compiler_params=pltpu.CompilerParams(vmem_limit_bytes=VMEM_LIMIT),
+        name=name,
+    )(which, shared, own_lo, own_hi, weight)
+
+
+def dealt_body(
+    queries,
+    window_keys,
+    window_values,
+    context_keys,
+    context_values,
+    block_group,
+    sees,
+    out_weight,
+    gate,
+):
+    tok_rows = queries.shape[0]
+    ctx_rows = context_keys.shape[0]
+    tm_count = lax.axis_size("tm")
+    own_index = lax.axis_index("tm")
+    core = lax.axis_index("head")
+    side = own_index % 2
+    half_q, half_c = tok_rows // 2, ctx_rows // 2
+
+    shared, own = pack(queries, context_keys, window_keys, context_values, window_values)
+    shared = lax.all_to_all(shared, "tm", 0, 0, tiled=True)
+    own = lax.all_to_all(own, "tm", 0, 0, tiled=True)
+
+    table = sees.astype(jnp.float32)
+    groups = jnp.arange(sees.shape[0], dtype=jnp.int32)
+    picks = (block_group[:, None] == groups[None, :]).astype(jnp.float32)
+    ctx_blocks = ctx_rows * tm_count // BLOCK
+    can_see = picks[ctx_blocks:] @ table @ picks.T
+    bias_blocks = jnp.where(can_see > 0.5, jnp.float32(0.0), jnp.float32(MASKED))
+    n_query_blocks = bias_blocks.shape[0]
+
+    def by_device(x, rows):
+        return x.reshape(n_query_blocks, tm_count, rows // BLOCK)
+
+    ctx_part = by_device(bias_blocks[:, :ctx_blocks], ctx_rows)
+    win_part = by_device(bias_blocks[:, ctx_blocks:], tok_rows)
+    spread = lambda x: jnp.broadcast_to(
+        x.reshape(x.shape[0], -1)[:, :, None], (x.shape[0], x[0].size, BLOCK)
+    ).reshape(x.shape[0], -1)
+    own_bias = spread(jnp.concatenate([ctx_part, win_part], axis=2))
+    own_bias = own_bias.reshape(tm_count, 2, half_q // BLOCK, -1)
+    own_bias_lo = own_bias[:, 0].reshape(n_query_blocks // 2, -1)
+    own_bias_hi = own_bias[:, 1].reshape(n_query_blocks // 2, -1)
+
+    def one_half(x, rows, which):
+        blocks = rows // 2 // BLOCK
+        return lax.dynamic_slice_in_dim(x, which * blocks, blocks, 2)
+
+    shared_rows = []
+    for which in (side, 1 - side):
+        shared_rows.append(
+            jnp.concatenate(
+                [one_half(ctx_part, ctx_rows, which), one_half(win_part, tok_rows, which)], axis=2
+            ).reshape(n_query_blocks, -1)
+        )
+    shared_blocks = jnp.concatenate(shared_rows, axis=1).reshape(
+        tm_count, tok_rows // BLOCK, -1
+    )
+    shared_blocks = lax.dynamic_slice_in_dim(
+        shared_blocks, side * (half_q // BLOCK), half_q // BLOCK, 1
+    ).reshape(n_query_blocks // 2, -1)
+    shared_bias = spread(shared_blocks)
+
+    theirs = lax.ppermute(shared[:, half_q:, :], "tm", [(i, i ^ 1) for i in range(tm_count)])
+
+    half_kv, full_kv = half_c + half_q, ctx_rows + tok_rows
+    shared_out = attend(
+        (shared, theirs),
+        (
+            (half_q, half_q + half_kv, half_q + half_kv, half_q + 2 * half_kv),
+            (0, half_kv, half_kv, 2 * half_kv),
+        ),
+        shared_bias,
+        0,
+        half_q,
+        4 * BLOCK,
+        "attend_shared",
+    )
+    shared_out = lax.all_to_all(shared_out, "tm", 0, 0, tiled=True)
+    own_source = ((tok_rows, tok_rows + full_kv, tok_rows + full_kv, tok_rows + 2 * full_kv),)
+    own_lo = attend((own,), own_source, own_bias_lo, 0, half_q, 4 * BLOCK, "attend_lo")
+    own_lo = lax.all_to_all(own_lo, "tm", 0, 0, tiled=True)
+    own_hi = attend((own,), own_source, own_bias_hi, half_q, half_q, 4 * BLOCK, "attend_hi")
+    own_hi = lax.all_to_all(own_hi, "tm", 0, 0, tiled=True)
+
+    columns = gate.shape[0]
+    other = (1 - core).astype(jnp.int32).reshape(1)
+    mine = core.astype(jnp.int32).reshape(1)
+    sent = project(
+        shared_out, own_lo, own_hi, out_weight, other, columns, jnp.bfloat16, "project_theirs"
+    )
+    got = lax.ppermute(sent, "head", [(0, 1), (1, 0)])
+    kept = project(
+        shared_out, own_lo, own_hi, out_weight, mine, columns, jnp.float32, "project_mine"
+    )
+    return (gate[None, :] * (kept + got.astype(jnp.float32))).astype(jnp.bfloat16)
+
+
+def body(queries, window_keys, window_values, context_keys, *rest):
+    tm_count = lax.axis_size("tm")
+    local_heads = queries.shape[1] // HD
+    halves = (queries.shape[0] // 2, context_keys.shape[0] // 2)
+    dealt = (
+        2 * local_heads == 3 * tm_count
+        and lax.axis_size("head") == 2
+        and all(h % BLOCK == 0 for h in halves)
+        and halves[0] * tm_count % (4 * BLOCK) == 0
+    )
+    chosen = dealt_body if dealt else gathered_body
+    return chosen(queries, window_keys, window_values, context_keys, *rest)
+
+
 def solution(mesh):
     placed = (
         P("tm", "head"),

time: 678 us -> 184 us (0.27)
  waiting for transfers between devices: 537 us -> 45.5 us
  matrix products: 70 us -> 0.24 us
  Pallas kernels: 0 us -> 56.4 us
  blocking collectives: 0 us -> 40.9 us
  starting transfers between devices: 0.35 us -> 31.3 us
  other arithmetic: 27.5 us -> 1.35 us
  local copies, waits for them, and re-layouts: 28.7 us -> 7.13 us
  between operations: 13.3 us -> 0.2 us
    unnamed x7 -> x0, waiting for transfers between devices: 240 us -> none
    all_gather x1 -> x0, waiting for transfers between devices: 188 us -> none  [body(): all_queries = lax.all_gather(queries, 'tm', axis=0, tiled=True)]
    pmax x1 -> x0, waiting for transfers between devices: 100 us -> none  [body(): lax.pmax(jnp.max(scores, axis=-1).astype(jnp.bfloat16), 'tm')]
    dot_general x7 -> x1, matrix products: 70 us -> 0.24 us  [dealt_body(): can_see = picks[ctx_blocks:] @ table @ picks.T]
    pallas_call x0 -> x6, Pallas kernels: none -> 56.4 us  [the longest x3 28.7 us: attend(): pl.pallas_call(functools.partial(attend_kernel, q_from, q_rows, sources,...]
    all_to_all x0 -> x1, blocking collectives: none -> 40.9 us  [dealt_body(): shared = lax.all_to_all(shared, 'tm', 0, 0, tiled=True)]
    ppermute x0 -> x2, waiting for transfers between devices: none -> 37 us  [the longest x1 37 us: dealt_body(): lax.ppermute(shared[:, half_q:, :], 'tm', [(i, i ^ 1) for i in range(tm_c...]
    all_to_all x0 -> x4, starting transfers between devices: none -> 29.5 us  [the longest x1 11.2 us: dealt_body(): shared_out = lax.all_to_all(shared_out, 'tm', 0, 0, tiled=True)]
  transfers between devices with their start and end apart: 5 -> 6, of which waited for: 5 -> 2; matrix products, arithmetic and copies ran while one was open for 8% -> 4% of each run, Pallas kernels for 0% -> 21%
where the time goes in v1:
time: 184 us; the launch traced here: 183 us
  Pallas kernels  56.4 us (31%)
  waiting for transfers between devices  45.5 us (25%)
  blocking collectives  40.9 us (22%)
  starting transfers between devices  31.3 us (17%)
  local copies, waits for them, and re-layouts  7.13 us (4%)
    all_to_all x1, blocking collectives, dealt_body(): shared = lax.all_to_all(shared, 'tm', 0, 0, tiled=True)  40.9 us
    ppermute x1, waiting for transfers between devices, dealt_body(): lax.ppermute(shared[:, half_q:, :], 'tm', [(i, i ^ 1) for i in range(tm_c...  37 us
    pallas_call x3, Pallas kernels, attend(): pl.pallas_call(functools.partial(attend_kernel, q_from, q_rows, sources,...  28.7 us
    pallas_call x2, Pallas kernels, project(): pl.pallas_call(project_kernel, grid_spec=pltpu.PrefetchScalarGridSpec(num...  20.9 us
    all_to_all x1, starting transfers between devices, dealt_body(): shared_out = lax.all_to_all(shared_out, 'tm', 0, 0, tiled=True)  11.2 us
    all_to_all x1, waiting for transfers between devices, dealt_body(): own_hi = lax.all_to_all(own_hi, 'tm', 0, 0, tiled=True)  8.5 us
    all_to_all x1, starting transfers between devices, dealt_body(): own_lo = lax.all_to_all(own_lo, 'tm', 0, 0, tiled=True)  6.91 us
    all_to_all x1, starting transfers between devices, dealt_body(): own_hi = lax.all_to_all(own_hi, 'tm', 0, 0, tiled=True)  6.9 us
  transfers between devices with their start and end apart: 6, of which 2 were waited for; matrix products, arithmetic and copies ran while one was open for 4% of the time, Pallas kernels for 21%

profile of v1, /device:TPU:0, one launch (start us, length us, event | category | flops | bytes accessed | tf_op | source)
XLA Modules:
  0.0 183.0 jit_solution(12153168990711164549)
XLA Ops:
  0.0 6.8 %pack.1 = (bf16[16,320,128]{2,1,0:T(8,128)(2,1)}, bf16[16,640,128]{2,1,0:T(8,128)(2,1)}) custom-call(bf16[128,3072]{1,0:T(8,128)(2,1)} %q_ref.1, bf16[128,3072]{1,0:T(8,128)(2,1)} %ck_ref.1, bf16[128,3072]{1,0:T(8,128)(2,1)} %wk_ref.1, bf16[128,3072]{1,0:T(8,128)(2,1)} %cv_ref.1, bf16[128,3072]{1,0:T(8,128)(2,1)} %wv_ref.1), custom_call_target="tpu_custom_call" | custom-call | tf_op jit(solution)/shard_map/pack/pallas_call | solution.py:123
  6.8 40.9 %all_to_all.25.refs_0_ = bf16[16,320,128]{2,1,0:T(8,128)(2,1)S(1)} all-to-all(bf16[16,320,128]{2,1,0:T(8,128)(2,1)} %get-tuple-element.7), channel_id=1, replica_groups=mesh['tm'=16,'head'=2] {'tm'}, dimensions={0} | all-to-all | bytes 2621440 | tf_op jit(solution)/shard_map/all_to_all | solution.py:271
  47.6 4.5 %all-to-all-start.2 = ((bf16[16,640,128]{2,1,0:T(8,128)(2,1)}), bf16[16,640,128]{2,1,0:T(8,128)(2,1)}, u32[]{:S(2)}, u32[]{:S(2)}) async-start(bf16[16,640,128]{2,1,0:T(8,128)(2,1)} %get-tuple-element.8), calls=%async_computation.2 | async-start | bytes 5242880 | tf_op jit(solution)/shard_map/all_to_all | solution.py:272
  52.1 0.0 copy-start.2
  52.1 0.0 copy-start.1
  52.1 1.1 slice.24
  53.2 1.7 collective-permute-start
  54.9 0.0 copy-done.2
  55.0 0.1 iota_compare_fusion
  55.0 0.0 copy-done.1
  55.0 0.2 fusion.6
  55.3 0.1 fusion.14
  55.3 0.1 copy.11
  55.4 0.1 copy.10
  55.6 0.2 reshape.27
  55.7 0.2 copy.15
  56.0 0.2 reshape.28
  56.1 0.2 copy.16
  56.3 0.1 fusion.11
  56.4 0.2 broadcast_in_dim.28
  56.6 0.2 reshape_reshape.6.refs_2_
  56.9 0.1 copy.14
  56.9 1.3 broadcast_in_dim.30
  58.3 1.7 reshape_reshape.7
  60.0 37.0 %collective-permute-done.refs_1_ = bf16[16,256,128]{2,1,0:T(8,128)(2,1)S(1)} collective-permute-done((bf16[16,256,128]{2,1,0:T(8,128)(2,1)}, bf16[16,256,128]{2,1,0:T(8,128)(2,1)S(1)}, u32[]{:S(2)}, u32[]{:S(2)}) %collective-permute-start) | collective-permute-done | bytes 1048608 | tf_op jit(solution)/shard_map/ppermute | solution.py:314
  97.0 8.4 %attend_shared.1 = bf16[16,64,128]{2,1,0:T(8,128)(2,1)} custom-call(bf16[16,320,128]{2,1,0:T(8,128)(2,1)S(1)} %all_to_all.25.refs_0_, bf16[16,256,128]{2,1,0:T(8,128)(2,1)S(1)} %collective-permute-done.refs_1_, f32[4,4,4096]{2,1,0:T(4,128)S(1)} %reshape_reshape.6.refs_2_), custom_call_target="tpu_custom_call" | custom-call | flops 4294967296 | bytes 4194304 | tf_op jit(solution)/shard_map/attend_shared/pallas_call | solution.py:187
  105.4 0.0 all-to-all-done.2.refs_0_
  105.4 11.2 %all-to-all-start.1 = ((bf16[16,64,128]{2,1,0:T(8,128)(2,1)}), bf16[16,64,128]{2,1,0:T(8,128)(2,1)S(1)}, u32[]{:S(2)}, u32[]{:S(2)}) async-start(bf16[16,64,128]{2,1,0:T(8,128)(2,1)} %attend_shared.1), calls=%async_computation.1 | async-start | bytes 524288 | tf_op jit(solution)/shard_map/all_to_all | solution.py:329
  116.7 1.4 slice_reduce_fusion
  118.0 0.1 reshape_reshape_squeeze.6.refs_1_
  118.1 10.2 %attend_lo.1 = bf16[16,64,128]{2,1,0:T(8,128)(2,1)} custom-call(bf16[16,640,128]{2,1,0:T(8,128)(2,1)} %all-to-all-done.2.refs_0_, f32[4,4,4096]{2,1,0:T(4,128)S(1)} %reshape_reshape_squeeze.6.refs_1_), custom_call_target="tpu_custom_call" | custom-call | flops 4294967296 | bytes 4194304 | tf_op jit(solution)/shard_map/attend_lo/pallas_call | solution.py:187
  128.3 0.0 all-to-all-done.1.shared_ref
  128.3 6.9 %all-to-all-start.3 = ((bf16[16,64,128]{2,1,0:T(8,128)(2,1)}), bf16[16,64,128]{2,1,0:T(8,128)(2,1)S(1)}, u32[]{:S(2)}, u32[]{:S(2)}) async-start(bf16[16,64,128]{2,1,0:T(8,128)(2,1)} %attend_lo.1), calls=%async_computation.3 | async-start | bytes 524288 | tf_op jit(solution)/shard_map/all_to_all | solution.py:332
  135.2 0.1 reshape_reshape_squeeze.7.refs_1_
  135.3 10.2 %attend_hi.1 = bf16[16,64,128]{2,1,0:T(8,128)(2,1)} custom-call(bf16[16,640,128]{2,1,0:T(8,128)(2,1)} %all-to-all-done.2.refs_0_, f32[4,4,4096]{2,1,0:T(4,128)S(1)} %reshape_reshape_squeeze.7.refs_1_), custom_call_target="tpu_custom_call" | custom-call | flops 4294967296 | bytes 4194304 | tf_op jit(solution)/shard_map/attend_hi/pallas_call | solution.py:187
  145.5 0.0 all-to-all-done.3.own_lo_ref
  145.5 6.9 %all-to-all-start.4 = ((bf16[16,64,128]{2,1,0:T(8,128)(2,1)}), bf16[16,64,128]{2,1,0:T(8,128)(2,1)S(1)}, u32[]{:S(2)}, u32[]{:S(2)}) async-start(bf16[16,64,128]{2,1,0:T(8,128)(2,1)} %attend_hi.1), calls=%async_computation.4 | async-start | bytes 524288 | tf_op jit(solution)/shard_map/all_to_all | solution.py:334
  152.4 8.5 %all-to-all-done.4.own_hi_ref = bf16[16,64,128]{2,1,0:T(8,128)(2,1)S(1)} async-done(((bf16[16,64,128]{2,1,0:T(8,128)(2,1)}), bf16[16,64,128]{2,1,0:T(8,128)(2,1)S(1)}, u32[]{:S(2)}, u32[]{:S(2)}) %all-to-all-start.4) | async-done | bytes 262176 | tf_op jit(solution)/shard_map/all_to_all | solution.py:334
  160.9 10.4 %project_theirs.1 = bf16[128,3072]{1,0:T(8,128)(2,1)S(1)} custom-call(s32[1]{0:T(128)} %bitcast.5.which_ref, bf16[16,64,128]{2,1,0:T(8,128)(2,1)S(1)} %all-to-all-done.1.shared_ref, bf16[16,64,128]{2,1,0:T(8,128)(2,1)S(1)} %all-to-all-done.3.own_lo_ref, bf16[16,64,128]{2,1,0:T(8,128)(2,1)S(1)} %all-to-all-done.4.own_hi_ref, bf16[3072,6144]{1,0:T(8,128)(2,1)} %w_ref.3), custom_call_target="tpu_custom_call" | custom-call | flops 2415919104 | bytes 18874368 | tf_op jit(solution)/shard_map/project_theirs/pallas_call | solution.py:226
  171.3 0.1 collective-permute-start.1
  171.4 0.0 copy-start
  171.4 10.5 %project_mine.1 = f32[128,3072]{1,0:T(8,128)S(1)} custom-call(s32[1]{0:T(128)} %bitcast.which_ref, bf16[16,64,128]{2,1,0:T(8,128)(2,1)S(1)} %all-to-all-done.1.shared_ref, bf16[16,64,128]{2,1,0:T(8,128)(2,1)S(1)} %all-to-all-done.3.own_lo_ref, bf16[16,64,128]{2,1,0:T(8,128)(2,1)S(1)} %all-to-all-done.4.own_hi_ref, bf16[3072,6144]{1,0:T(8,128)(2,1)} %w_ref.3), custom_call_target="tpu_custom_call" | custom-call | flops 2415919104 | bytes 18874368 | tf_op jit(solution)/shard_map/project_mine/pallas_call | solution.py:226
  181.9 0.0 collective-permute-done.1
  181.9 0.0 copy-done
  181.9 1.1 multiply_convert_fusion
  (4 shorter events, 0.1 us)
Async XLA Ops:
  47.6 57.8 %all-to-all-start.2 = ((bf16[16,640,128]{2,1,0:T(8,128)(2,1)}), bf16[16,640,128]{2,1,0:T(8,128)(2,1)}, u32[]{:S(2)}, u32[]{:S(2)}) async-start(bf16[16,640,128]{2,1,0:T(8,128)(2,1)} %get-tuple-element.8), calls=%async_computation.2 | async-start | bytes 5242880 | tf_op jit(solution)/shard_map/all_to_all | solution.py:272
  52.1 2.8 %copy-start.2 = (s32[64]{0:T(128)S(1)}, s32[64]{0:T(128)}, u32[]{:S(2)}) copy-start(s32[64]{0:T(128)} %param.14) | copy-start | bytes 772
  52.1 2.9 %copy-start.1 = (s32[16,16]{1,0:T(8,128)S(1)}, s32[16,16]{1,0:T(8,128)}, u32[]{:S(2)}) copy-start(s32[16,16]{1,0:T(8,128)} %param.15) | copy-start | bytes 3076
  53.2 43.8 %collective-permute-start = (bf16[16,256,128]{2,1,0:T(8,128)(2,1)}, bf16[16,256,128]{2,1,0:T(8,128)(2,1)S(1)}, u32[]{:S(2)}, u32[]{:S(2)}) collective-permute-start(bf16[16,256,128]{2,1,0:T(8,128)(2,1)} %slice.24), channel_id=1, source_target_pairs={{0,2},{2,0},{4,6},{6,4},{8,10},{10,8},{12,14},{14,12},{16,18},{18,... | collective-permute-start | bytes 3145736 | tf_op jit(solution)/shard_map/ppermute | solution.py:314
  105.4 22.8 %all-to-all-start.1 = ((bf16[16,64,128]{2,1,0:T(8,128)(2,1)}), bf16[16,64,128]{2,1,0:T(8,128)(2,1)S(1)}, u32[]{:S(2)}, u32[]{:S(2)}) async-start(bf16[16,64,128]{2,1,0:T(8,128)(2,1)} %attend_shared.1), calls=%async_computation.1 | async-start | bytes 524288 | tf_op jit(solution)/shard_map/all_to_all | solution.py:329
  128.3 17.2 %all-to-all-start.3 = ((bf16[16,64,128]{2,1,0:T(8,128)(2,1)}), bf16[16,64,128]{2,1,0:T(8,128)(2,1)S(1)}, u32[]{:S(2)}, u32[]{:S(2)}) async-start(bf16[16,64,128]{2,1,0:T(8,128)(2,1)} %attend_lo.1), calls=%async_computation.3 | async-start | bytes 524288 | tf_op jit(solution)/shard_map/all_to_all | solution.py:332
  145.5 15.4 %all-to-all-start.4 = ((bf16[16,64,128]{2,1,0:T(8,128)(2,1)}), bf16[16,64,128]{2,1,0:T(8,128)(2,1)S(1)}, u32[]{:S(2)}, u32[]{:S(2)}) async-start(bf16[16,64,128]{2,1,0:T(8,128)(2,1)} %attend_hi.1), calls=%async_computation.4 | async-start | bytes 524288 | tf_op jit(solution)/shard_map/all_to_all | solution.py:334
  171.3 10.6 %collective-permute-start.1 = (bf16[128,3072]{1,0:T(8,128)(2,1)S(1)}, bf16[128,3072]{1,0:T(8,128)(2,1)S(1)}, u32[]{:S(2)}, u32[]{:S(2)}) collective-permute-start(bf16[128,3072]{1,0:T(8,128)(2,1)S(1)} %project_theirs.1), channel_id=1, source_target_pairs={{0,1},{1,0},{2,3},{3,2},{4,5},{5,4},{6,7},{7,6},{8,9},{9,8},{10,11... | collective-permute-start | bytes 2359304 | tf_op jit(solution)/shard_map/ppermute | solution.py:342
  171.4 10.5 %copy-start = (f32[3072]{0:T(1024)S(1)}, f32[3072]{0:T(1024)}, u32[]{:S(2)}) copy-start(f32[3072]{0:T(1024)} %param.17) | copy-start | bytes 36868

commit v2 on v0

--- a/solution.py
+++ b/solution.py
@@ -1,10 +1,22 @@
+import functools
+import math
+
 import jax
 import jax.numpy as jnp
 from jax import lax
+from jax.experimental import pallas as pl
+from jax.experimental.pallas import tpu as pltpu
 from jax.sharding import PartitionSpec as P
 
 HD = 128
 BLOCK = 64
+MASKED = -1e30
+VMEM_LIMIT = 40 * 1024 * 1024
+TILE_ROWS = 4 * BLOCK
+KEY_CHUNK = 256
+ACCUMULATORS = 2
+PROJECT_COLUMNS = 1024
+PROJECT_PIECES = 6
 
 
 def group_rows(positions, group_table, group_count):
@@ -18,7 +30,7 @@
     )
 
 
-def body(
+def gathered_body(
     queries,
     window_keys,
     window_values,
@@ -95,6 +107,325 @@
     return (gate[None, :] * summed).astype(jnp.bfloat16)
 
 
+def pack_kernel(whole, *refs):
+    n = (len(refs) - 2) // 2
+    in_refs, out_ref, held, sems = refs[:n], refs[n], refs[n + 1 : -1], refs[-1]
+    copies = [pltpu.make_async_copy(x, y, sems.at[i]) for i, (x, y) in enumerate(zip(in_refs, held))]
+    for copy in copies:
+        copy.start()
+    at = 0
+    for copy, ref in zip(copies, held):
+        copy.wait()
+        rows = ref.shape[0]
+        half = rows // 2
+        for j in range(ref.shape[1] // (3 * HD)):
+            for side in range(2):
+                if whole:
+                    head = 3 * j + 2 * side
+                    out_ref[2 * j + side, at : at + rows, :] = ref[:, head * HD : (head + 1) * HD]
+                else:
+                    head = 3 * j + 1
+                    out_ref[2 * j + side, at : at + half, :] = ref[
+                        side * half : (side + 1) * half, head * HD : (head + 1) * HD
+                    ]
+        at += rows if whole else half
+
+
+def pack(arrays, whole, name):
+    groups = arrays[0].shape[1] // (3 * HD)
+    rows = [x.shape[0] for x in arrays]
+    total = sum(rows) if whole else sum(rows) // 2
+    return pl.pallas_call(
+        functools.partial(pack_kernel, whole),
+        in_specs=[pl.BlockSpec(memory_space=pl.ANY) for _ in arrays],
+        out_specs=pl.BlockSpec(memory_space=pltpu.VMEM),
+        out_shape=jax.ShapeDtypeStruct((2 * groups, total, HD), arrays[0].dtype),
+        scratch_shapes=[pltpu.VMEM(x.shape, x.dtype) for x in arrays]
+        + [pltpu.SemaphoreType.DMA((len(arrays),))],
+        cost_estimate=pl.CostEstimate(
+            flops=1 << 29, bytes_accessed=8 * 1024 * 1024, transcendentals=0
+        ),
+        compiler_params=pltpu.CompilerParams(vmem_limit_bytes=VMEM_LIMIT),
+        name=name,
+    )(*arrays)
+
+
+def attend_kernel(q_rows, keys_at, scale, carried, *refs):
+    if carried:
+        q_ref, kv_ref, bias_ref, mine_ref, theirs_ref, out_ref, k_all, v_all, kept_a, kept_b = refs
+    else:
+        q_ref, kv_ref, bias_ref, out_ref, k_all, v_all, kept_a, kept_b = refs
+    keys = k_all.shape[0]
+    chips = TILE_ROWS // q_rows
+    runs = TILE_ROWS // BLOCK
+    tiles = q_ref.shape[0] // chips
+    half = q_rows // 2
+
+    k_lo, k_hi, v_lo, v_hi = keys_at
+    count = kv_ref.shape[0]
+    k_all[:, :HD] = kv_ref[:, k_lo:k_hi, :].reshape(keys, HD)
+    blocks = keys // BLOCK
+    k_all[:, HD:] = (
+        jnp.broadcast_to(bias_ref[...][:, None, :], (blocks, BLOCK, HD))
+        .reshape(keys, HD)
+        .astype(jnp.bfloat16)
+    )
+    some = v_hi - v_lo
+    for i in range(count):
+        v_all[:, i * some : (i + 1) * some] = kv_ref[i, v_lo:v_hi, :].T
+
+    def finish(pair, odd, peak, total, numer):
+        total = jnp.sum(total, axis=0, keepdims=True)
+        numer = numer / total
+        tile = 2 * pair + odd
+        if not carried:
+            out_ref[tile, :HD, :] = numer
+            out_ref[tile, HD:, :] = jnp.broadcast_to(peak + jnp.log2(total), (8, TILE_ROWS))
+            return
+        side = TILE_ROWS // 2
+        mine = mine_ref[pair, :, odd * side : (odd + 1) * side]
+        theirs = theirs_ref[pair, :, odd * side : (odd + 1) * side]
+        mine_log, their_log = mine[HD : HD + 1, :], theirs[HD : HD + 1, :]
+        top = jnp.maximum(mine_log, their_log)
+        mine_part, their_part = jnp.exp2(mine_log - top), jnp.exp2(their_log - top)
+        joined = (mine_part * mine[:HD, :] + their_part * theirs[:HD, :]) / (mine_part + their_part)
+        here = pl.ds(tile * chips, chips)
+        out_ref[here, :half, :] = joined.T.astype(out_ref.dtype).reshape(chips, half, HD)
+        out_ref[here, half:, :] = numer.T.astype(out_ref.dtype).reshape(chips, q_rows, HD)
+
+    def advance(ahead, ahead_kept, pair, odd, peak, kept):
+        if ahead is not None:
+            q = q_ref[pl.ds(ahead * chips, chips), :q_rows, :].reshape(TILE_ROWS, HD).T
+            row = lax.broadcasted_iota(jnp.int32, (HD, TILE_ROWS), 0)
+            col = lax.broadcasted_iota(jnp.int32, (HD, TILE_ROWS), 1)
+            run = (row == ahead * runs + col // BLOCK).astype(jnp.float32).astype(jnp.bfloat16)
+            q = jnp.concatenate([q, run], axis=0)
+            new_peak = jnp.full((8, TILE_ROWS), MASKED, jnp.float32)
+        if kept is not None:
+            total = jnp.zeros((8, TILE_ROWS), jnp.float32)
+            numer = [jnp.zeros((HD, TILE_ROWS), jnp.float32) for _ in range(ACCUMULATORS)]
+        for turn, at in enumerate(range(0, keys, KEY_CHUNK)):
+            if ahead is not None:
+                scores = jnp.dot(
+                    k_all[at : at + KEY_CHUNK, :], q, preferred_element_type=jnp.float32
+                )
+                ahead_kept[at : at + KEY_CHUNK, :] = scores
+                new_peak = jnp.maximum(new_peak, jnp.max(scores.reshape(-1, 8, TILE_ROWS), axis=0))
+            if kept is not None:
+                weights = jnp.exp2(kept[at : at + KEY_CHUNK, :] * scale - peak)
+                total = total + jnp.sum(weights.reshape(-1, 8, TILE_ROWS), axis=0)
+                numer[turn % ACCUMULATORS] += jnp.dot(
+                    v_all[:, at : at + KEY_CHUNK],
+                    weights.astype(jnp.bfloat16),
+                    preferred_element_type=jnp.float32,
+                )
+        if kept is not None:
+            finish(pair, odd, peak, total, functools.reduce(jnp.add, numer))
+        if ahead is not None:
+            return jnp.max(new_peak, axis=0, keepdims=True) * scale
+
+    peak = advance(0, kept_a, None, None, None, None)
+
+    def two(pair, peak):
+        peak = advance(2 * pair + 1, kept_b, pair, 0, peak, kept_a)
+        return advance(2 * pair + 2, kept_a, pair, 1, peak, kept_b)
+
+    last = tiles // 2 - 1
+    peak = lax.fori_loop(0, last, two, peak)
+    peak = advance(tiles - 1, kept_b, last, 0, peak, kept_a)
+    advance(None, None, last, 1, peak, kept_b)
+
+
+def attend(q, q_rows, kv, keys_at, bias, carried, name):
+    count = q.shape[0]
+    chips = TILE_ROWS // q_rows
+    keys = count * (keys_at[1] - keys_at[0])
+    scale = math.log2(math.e) / math.sqrt(HD)
+    work = count * q_rows * keys
+    if carried:
+        out_shape = jax.ShapeDtypeStruct((count, q_rows + q_rows // 2, HD), jnp.bfloat16)
+    else:
+        out_shape = jax.ShapeDtypeStruct((count // chips, HD + 8, TILE_ROWS), jnp.float32)
+    vmem = pl.BlockSpec(memory_space=pltpu.VMEM)
+    return pl.pallas_call(
+        functools.partial(attend_kernel, q_rows, keys_at, scale, bool(carried)),
+        in_specs=[vmem] * (3 + len(carried)),
+        out_specs=vmem,
+        out_shape=out_shape,
+        scratch_shapes=[
+            pltpu.VMEM((keys, 2 * HD), jnp.bfloat16),
+            pltpu.VMEM((HD, keys), jnp.bfloat16),
+            pltpu.VMEM((keys, TILE_ROWS), jnp.float32),
+            pltpu.VMEM((keys, TILE_ROWS), jnp.float32),
+        ],
+        cost_estimate=pl.CostEstimate(
+            flops=8 * work * HD, bytes_accessed=4 * 1024 * 1024, transcendentals=work
+        ),
+        compiler_params=pltpu.CompilerParams(vmem_limit_bytes=VMEM_LIMIT),
+        name=name,
+    )(q, kv, bias, *carried)
+
+
+def project_kernel(half, which_ref, attended_ref, w_ref, out_ref, left, held, acc, sems):
+    pairs = attended_ref.shape[0] // 2
+    columns = out_ref.shape[1]
+    pieces = sems.shape[0]
+    depth = w_ref.shape[0] // pieces
+    base = pl.multiple_of(which_ref[0] * columns, HD)
+    copies = [
+        pltpu.make_async_copy(
+            w_ref.at[pl.ds(i * depth, depth), pl.ds(base, columns)],
+            held.at[pl.ds(i * depth, depth), :],
+            sems.at[i],
+        )
+        for i in range(pieces)
+    ]
+    for copy in copies:
+        copy.start()
+    for j in range(pairs):
+        at = 3 * j * HD
+        left[:, at : at + HD] = attended_ref[2 * j, half:, :]
+        left[:half, at + HD : at + 2 * HD] = attended_ref[2 * j, :half, :]
+        left[half:, at + HD : at + 2 * HD] = attended_ref[2 * j + 1, :half, :]
+        left[:, at + 2 * HD : at + 3 * HD] = attended_ref[2 * j + 1, half:, :]
+    for i, copy in enumerate(copies):
+        copy.wait()
+        rows = slice(i * depth, (i + 1) * depth)
+        for n in range(0, columns, PROJECT_COLUMNS):
+            here = slice(n, n + PROJECT_COLUMNS)
+            part = jnp.dot(left[:, rows], held[rows, here], preferred_element_type=jnp.float32)
+            if i > 0:
+                part = acc[:, here] + part
+            if i + 1 < pieces:
+                acc[:, here] = part
+            else:
+                out_ref[:, here] = part.astype(out_ref.dtype)
+
+
+def project(attended, half, weight, which, columns, dtype, name):
+    vmem = pl.BlockSpec(memory_space=pltpu.VMEM)
+    return pl.pallas_call(
+        functools.partial(project_kernel, half),
+        in_specs=[
+            pl.BlockSpec(memory_space=pltpu.SMEM),
+            vmem,
+            pl.BlockSpec(memory_space=pl.ANY),
+        ],
+        out_specs=vmem,
+        out_shape=jax.ShapeDtypeStruct((2 * half, columns), dtype),
+        scratch_shapes=[
+            pltpu.VMEM((2 * half, weight.shape[0]), jnp.bfloat16),
+            pltpu.VMEM((weight.shape[0], columns), jnp.bfloat16),
+            pltpu.VMEM((2 * half, columns), jnp.float32),
+            pltpu.SemaphoreType.DMA((PROJECT_PIECES,)),
+        ],
+        cost_estimate=pl.CostEstimate(
+            flops=4 * half * weight.shape[0] * columns,
+            bytes_accessed=2 * weight.shape[0] * columns,
+            transcendentals=0,
+        ),
+        compiler_params=pltpu.CompilerParams(vmem_limit_bytes=VMEM_LIMIT),
+        name=name,
+    )(which, attended, weight)
+
+
+def dealt_body(
+    queries,
+    window_keys,
+    window_values,
+    context_keys,
+    context_values,
+    block_group,
+    sees,
+    out_weight,
+    gate,
+):
+    tok_rows = queries.shape[0]
+    ctx_rows = context_keys.shape[0]
+    tm_count = lax.axis_size("tm")
+    own_index = lax.axis_index("tm")
+    core = lax.axis_index("head")
+    side = own_index % 2
+    half_q, half_c = tok_rows // 2, ctx_rows // 2
+
+    arrays = [
+        pltpu.with_memory_space_constraint(x, pltpu.HBM)
+        for x in (queries, context_keys, window_keys, context_values, window_values)
+    ]
+    shared = lax.all_to_all(pack(arrays, False, "pack_shared"), "tm", 0, 0, tiled=True)
+    own = lax.all_to_all(pack(arrays, True, "pack_own"), "tm", 0, 0, tiled=True)
+
+    table = sees.astype(jnp.float32)
+    groups = jnp.arange(sees.shape[0], dtype=jnp.int32)
+    picks = (block_group[:, None] == groups[None, :]).astype(jnp.float32)
+    ctx_blocks = ctx_rows * tm_count // BLOCK
+    seen_by = picks @ table.T @ picks[ctx_blocks:].T
+    bias = jnp.where(seen_by > 0.5, jnp.float32(0.0), jnp.float32(MASKED))
+    n_query_blocks = bias.shape[1]
+    bias = jnp.concatenate(
+        [
+            bias[:ctx_blocks].reshape(tm_count, -1, n_query_blocks),
+            bias[ctx_blocks:].reshape(tm_count, -1, n_query_blocks),
+        ],
+        axis=1,
+    )
+    pad = lambda x: jnp.pad(x, ((0, 0), (0, HD - x.shape[1])))
+    own_bias = pad(bias.reshape(-1, n_query_blocks))
+    c_blocks, q_blocks = half_c // BLOCK, half_q // BLOCK
+    near = jnp.where(
+        side == 0,
+        jnp.concatenate(
+            [bias[:, :c_blocks], bias[:, 2 * c_blocks : 2 * c_blocks + q_blocks]], axis=1
+        ),
+        jnp.concatenate(
+            [bias[:, c_blocks : 2 * c_blocks], bias[:, 2 * c_blocks + q_blocks :]], axis=1
+        ),
+    ).reshape(-1, tm_count, 2, q_blocks)
+    flat = lambda x: pad(x.reshape(x.shape[0], -1))
+    lo, hi = flat(near[:, :, 0]), flat(near[:, :, 1])
+    my_bias = jnp.where(side == 0, lo, hi)
+    their_bias = jnp.where(side == 0, hi, lo)
+
+    swap = [(i, i ^ 1) for i in range(tm_count)]
+    half_kv, full_kv = half_c + half_q, ctx_rows + tok_rows
+    shared_at = (half_q, half_q + half_kv, half_q + half_kv, half_q + 2 * half_kv)
+    own_at = (tok_rows, tok_rows + full_kv, tok_rows + full_kv, tok_rows + 2 * full_kv)
+    their_q = lax.ppermute(shared[:, :half_q, :], "tm", swap)
+    mine = attend(shared, half_q, shared, shared_at, my_bias, (), "attend_mine")
+    theirs = attend(their_q, half_q, shared, shared_at, their_bias, (), "attend_theirs")
+    theirs = lax.ppermute(theirs, "tm", swap)
+    attended = attend(own, tok_rows, own, own_at, own_bias, (mine, theirs), "attend_own")
+    attended = lax.all_to_all(attended, "tm", 0, 0, tiled=True)
+
+    columns = gate.shape[0]
+    other = (1 - core).astype(jnp.int32).reshape(1)
+    this = core.astype(jnp.int32).reshape(1)
+    weight = pltpu.with_memory_space_constraint(out_weight, pltpu.HBM)
+    sent = project(attended, half_q, weight, other, columns, jnp.bfloat16, "project_theirs")
+    got = lax.ppermute(sent, "head", [(0, 1), (1, 0)])
+    kept = project(attended, half_q, weight, this, columns, jnp.float32, "project_mine")
+    return (gate[None, :] * (kept + got.astype(jnp.float32))).astype(jnp.bfloat16)
+
+
+def body(queries, window_keys, window_values, context_keys, *rest):
+    tm_count = lax.axis_size("tm")
+    local_heads = queries.shape[1] // HD
+    halves = (queries.shape[0] // 2, context_keys.shape[0] // 2)
+    dealt = (
+        2 * local_heads == 3 * tm_count
+        and lax.axis_size("head") == 2
+        and all(h % BLOCK == 0 for h in halves)
+        and TILE_ROWS % (2 * halves[0]) == 0
+        and halves[0] * tm_count % TILE_ROWS == 0
+        and tm_count * queries.shape[0] % (4 * TILE_ROWS) == 0
+        and queries.shape[1] % PROJECT_COLUMNS == 0
+        and queries.shape[1] % (PROJECT_PIECES * HD) == 0
+        and queries.shape[0] * tm_count // BLOCK <= HD
+    )
+    chosen = dealt_body if dealt else gathered_body
+    return chosen(queries, window_keys, window_values, context_keys, *rest)
+
+
 def solution(mesh):
     placed = (
         P("tm", "head"),

time: 678 us -> 158 us (0.23)
  waiting for transfers between devices: 537 us -> 77.6 us
  matrix products: 70 us -> 0.24 us
  Pallas kernels: 0 us -> 42.5 us
  starting transfers between devices: 0.35 us -> 29.5 us
  other arithmetic: 27.5 us -> 1.28 us
  local copies, waits for them, and re-layouts: 28.7 us -> 6.26 us
  between operations: 13.3 us -> 0.21 us
    unnamed x7 -> x0, waiting for transfers between devices: 240 us -> none
    all_gather x1 -> x0, waiting for transfers between devices: 188 us -> none  [body(): all_queries = lax.all_gather(queries, 'tm', axis=0, tiled=True)]
    pmax x1 -> x0, waiting for transfers between devices: 100 us -> none  [body(): lax.pmax(jnp.max(scores, axis=-1).astype(jnp.bfloat16), 'tm')]
    dot_general x7 -> x1, matrix products: 70 us -> 0.24 us  [dealt_body(): seen_by = picks @ table.T @ picks[ctx_blocks:].T]
    all_to_all x0 -> x3, waiting for transfers between devices: none -> 51.2 us  [the longest x1 25.7 us: dealt_body(): lax.all_to_all(pack(arrays, False, 'pack_shared'), 'tm', 0, 0, tiled=True)]
    pallas_call x0 -> x7, Pallas kernels: none -> 42.5 us  [the longest x3 21.3 us: attend(): pl.pallas_call(functools.partial(attend_kernel, q_rows, keys_at, scale, b...]
    all_to_all x0 -> x3, starting transfers between devices: none -> 27.2 us  [the longest x1 12 us: dealt_body(): attended = lax.all_to_all(attended, 'tm', 0, 0, tiled=True)]
    ppermute x0 -> x3, waiting for transfers between devices: none -> 26.4 us  [the longest x1 19.3 us: dealt_body(): theirs = lax.ppermute(theirs, 'tm', swap)]
  transfers between devices with their start and end apart: 5 -> 6, of which waited for: 5 -> 5; matrix products, arithmetic and copies ran while one was open for 8% -> 3% of each run, Pallas kernels for 0% -> 13%
where the time goes in v2:
time: 158 us
  waiting for transfers between devices  77.6 us (49%)
  Pallas kernels  42.5 us (27%)
  starting transfers between devices  29.5 us (19%)
  local copies, waits for them, and re-layouts  6.26 us (4%)
    all_to_all x1, waiting for transfers between devices, dealt_body(): lax.all_to_all(pack(arrays, False, 'pack_shared'), 'tm', 0, 0, tiled=True)  25.7 us
    pallas_call x3, Pallas kernels, attend(): pl.pallas_call(functools.partial(attend_kernel, q_rows, keys_at, scale, b...  21.3 us
    ppermute x1, waiting for transfers between devices, dealt_body(): theirs = lax.ppermute(theirs, 'tm', swap)  19.3 us
    all_to_all x1, waiting for transfers between devices, dealt_body(): attended = lax.all_to_all(attended, 'tm', 0, 0, tiled=True)  19 us
    pallas_call x2, Pallas kernels, project(): pl.pallas_call(functools.partial(project_kernel, half), in_specs=[pl.Bloc...  14.2 us
    all_to_all x1, starting transfers between devices, dealt_body(): attended = lax.all_to_all(attended, 'tm', 0, 0, tiled=True)  12 us
    all_to_all x1, starting transfers between devices, dealt_body(): lax.all_to_all(pack(arrays, False, 'pack_shared'), 'tm', 0, 0, tiled=True)  8.4 us
    ppermute x1, waiting for transfers between devices, dealt_body(): their_q = lax.ppermute(shared[:, :half_q, :], 'tm', swap)  7.06 us
  transfers between devices with their start and end apart: 6, of which 5 were waited for; matrix products, arithmetic and copies ran while one was open for 3% of the time, Pallas kernels for 13%

profile of v2, /device:TPU:0, one launch (start us, length us, event | category | flops | bytes accessed | tf_op | source)
XLA Modules:
  0.0 157.6 jit_solution(3232836569038316212)
XLA Ops:
  0.0 3.2 %pack_shared.1 = bf16[16,320,128]{2,1,0:T(8,128)(2,1)} custom-call(bf16[128,3072]{1,0:T(8,128)(2,1)} %refs_0_.3, bf16[128,3072]{1,0:T(8,128)(2,1)} %refs_1_.3, bf16[128,3072]{1,0:T(8,128)(2,1)} %refs_2_.3, bf16[128,3072]{1,0:T(8,128)(2,1)} %refs_3_.3, bf16[128,3072]{1,0:T(8,128)(2,1)} %refs_4_.3), custom_call_target="tpu_custom_call" | custom-call | flops 536870912 | bytes 8388608 | tf_op jit(solution)/shard_map/pack_shared/pallas_call | solution.py:138
  3.2 8.4 %all-to-all-start.1 = ((bf16[16,320,128]{2,1,0:T(8,128)(2,1)}), bf16[16,320,128]{2,1,0:T(8,128)(2,1)}, u32[]{:S(2)}, u32[]{:S(2)}) async-start(bf16[16,320,128]{2,1,0:T(8,128)(2,1)} %pack_shared.1), calls=%async_computation.1 | async-start | bytes 2621440 | tf_op jit(solution)/shard_map/all_to_all | solution.py:355
  11.6 3.7 %pack_own.1 = bf16[16,640,128]{2,1,0:T(8,128)(2,1)} custom-call(bf16[128,3072]{1,0:T(8,128)(2,1)} %refs_0_.3, bf16[128,3072]{1,0:T(8,128)(2,1)} %refs_1_.3, bf16[128,3072]{1,0:T(8,128)(2,1)} %refs_2_.3, bf16[128,3072]{1,0:T(8,128)(2,1)} %refs_3_.3, bf16[128,3072]{1,0:T(8,128)(2,1)} %refs_4_.3), custom_call_target="tpu_custom_call" | custom-call | flops 536870912 | bytes 8388608 | tf_op jit(solution)/shard_map/pack_own/pallas_call | solution.py:138
  15.4 0.0 copy-start.4
  15.4 0.0 copy-start.3
  15.4 25.7 %all-to-all-done.1.refs_0_.refs_1_ = bf16[16,320,128]{2,1,0:T(8,128)(2,1)} async-done(((bf16[16,320,128]{2,1,0:T(8,128)(2,1)}), bf16[16,320,128]{2,1,0:T(8,128)(2,1)}, u32[]{:S(2)}, u32[]{:S(2)}) %all-to-all-start.1) | async-done | bytes 1310752 | tf_op jit(solution)/shard_map/all_to_all | solution.py:355
  41.1 6.8 %all-to-all-start = ((bf16[16,640,128]{2,1,0:T(8,128)(2,1)}), bf16[16,640,128]{2,1,0:T(8,128)(2,1)S(1)}, u32[]{:S(2)}, u32[]{:S(2)}) async-start(bf16[16,640,128]{2,1,0:T(8,128)(2,1)} %pack_own.1), calls=%async_computation | async-start | bytes 5242880 | tf_op jit(solution)/shard_map/all_to_all | solution.py:356
  47.9 0.0 copy-done.4
  47.9 0.1 iota_compare_fusion
  48.0 0.0 copy-done.3
  48.0 0.2 fusion.6
  48.2 0.1 fusion.15
  48.3 0.1 copy.13
  48.4 0.1 copy.12
  48.5 0.2 select_n.46
  48.7 1.7 %slice.49 = bf16[16,64,128]{2,1,0:T(8,128)(2,1)} slice(bf16[16,320,128]{2,1,0:T(8,128)(2,1)} %all-to-all-done.1.refs_0_.refs_1_), slice={[0:16], [0:64], [0:128]} | slice | bytes 524288 | tf_op jit(solution)/shard_map/slice | solution.py:393
  50.4 1.9 %collective-permute-start = (bf16[16,64,128]{2,1,0:T(8,128)(2,1)}, bf16[16,64,128]{2,1,0:T(8,128)(2,1)S(1)}, u32[]{:S(2)}, u32[]{:S(2)}) collective-permute-start(bf16[16,64,128]{2,1,0:T(8,128)(2,1)} %slice.49), channel_id=1, source_target_pairs={{0,2},{2,0},{4,6},{6,4},{8,10},{10,8},{12,14},{14,12},{16,18},{18,... | collective-permute-start | bytes 786440 | tf_op jit(solution)/shard_map/ppermute | solution.py:393
  52.3 0.8 fusion.12
  53.1 1.2 copy.17
  54.3 0.3 copy.16
  54.6 7.1 %collective-permute-done.refs_0_ = bf16[16,64,128]{2,1,0:T(8,128)(2,1)S(1)} collective-permute-done((bf16[16,64,128]{2,1,0:T(8,128)(2,1)}, bf16[16,64,128]{2,1,0:T(8,128)(2,1)S(1)}, u32[]{:S(2)}, u32[]{:S(2)}) %collective-permute-start) | collective-permute-done | bytes 262176 | tf_op jit(solution)/shard_map/ppermute | solution.py:393
  61.7 4.9 %attend_theirs.1 = f32[4,136,256]{2,1,0:T(8,128)S(1)} custom-call(bf16[16,64,128]{2,1,0:T(8,128)(2,1)S(1)} %collective-permute-done.refs_0_, bf16[16,320,128]{2,1,0:T(8,128)(2,1)} %all-to-all-done.1.refs_0_.refs_1_, f32[32,128]{1,0:T(8,128)S(1)} %get-tuple-element.7.refs_2_), custom_call_target="tpu_custom_call" | custom-call | flops 2147483648 | bytes 4194304 | tf_op jit(solution)/shard_map/attend_theirs/pallas_call | solution.py:250
  66.6 0.3 collective-permute-start.1
  66.9 5.3 %attend_mine.1.refs_3_ = f32[4,136,256]{2,1,0:T(8,128)S(1)} custom-call(bf16[16,320,128]{2,1,0:T(8,128)(2,1)} %all-to-all-done.1.refs_0_.refs_1_, bf16[16,320,128]{2,1,0:T(8,128)(2,1)} %all-to-all-done.1.refs_0_.refs_1_, f32[32,128]{1,0:T(8,128)S(1)} %get-tuple-element.8.refs_2_), custom_call_target="tpu_custom_call" | custom-call | flops 2147483648 | bytes 4194304 | tf_op jit(solution)/shard_map/attend_mine/pallas_call | solution.py:250
  72.2 0.0 copy-start
  72.3 0.8 copy-done
  73.1 19.3 %collective-permute-done.1.refs_4_ = f32[4,136,256]{2,1,0:T(8,128)S(1)} collective-permute-done((f32[4,136,256]{2,1,0:T(8,128)S(1)}, f32[4,136,256]{2,1,0:T(8,128)S(1)}, u32[]{:S(2)}, u32[]{:S(2)}) %collective-permute-start.1) | collective-permute-done | bytes 557088 | tf_op jit(solution)/shard_map/ppermute | solution.py:396
  92.4 6.6 %all-to-all-done.refs_0_.refs_1_ = bf16[16,640,128]{2,1,0:T(8,128)(2,1)S(1)} async-done(((bf16[16,640,128]{2,1,0:T(8,128)(2,1)}), bf16[16,640,128]{2,1,0:T(8,128)(2,1)S(1)}, u32[]{:S(2)}, u32[]{:S(2)}) %all-to-all-start) | async-done | bytes 2621472 | tf_op jit(solution)/shard_map/all_to_all | solution.py:356
  98.9 0.0 copy-start.1
  98.9 1.1 copy-done.1
  100.0 11.1 %attend_own.1 = bf16[16,192,128]{2,1,0:T(8,128)(2,1)} custom-call(bf16[16,640,128]{2,1,0:T(8,128)(2,1)S(1)} %all-to-all-done.refs_0_.refs_1_, bf16[16,640,128]{2,1,0:T(8,128)(2,1)S(1)} %all-to-all-done.refs_0_.refs_1_, f32[64,128]{1,0:T(8,128)S(1)} %pad.11.refs_2_, f32[4,136,256]{2,1,0:T(8,128)S(1)} %copy-done.1, ...), custom_call_target="tpu_custom_call" | custom-call | flops 8589934592 | bytes 4194304 | tf_op jit(solution)/shard_map/attend_own/pallas_call | solution.py:250
  111.1 12.0 %all-to-all-start.2 = ((bf16[16,192,128]{2,1,0:T(8,128)(2,1)}), bf16[16,192,128]{2,1,0:T(8,128)(2,1)S(1)}, u32[]{:S(2)}, u32[]{:S(2)}) async-start(bf16[16,192,128]{2,1,0:T(8,128)(2,1)} %attend_own.1), calls=%async_computation.2 | async-start | bytes 1572864 | tf_op jit(solution)/shard_map/all_to_all | solution.py:398
  123.2 19.0 %all-to-all-done.2.attended_ref = bf16[16,192,128]{2,1,0:T(8,128)(2,1)S(1)} async-done(((bf16[16,192,128]{2,1,0:T(8,128)(2,1)}), bf16[16,192,128]{2,1,0:T(8,128)(2,1)S(1)}, u32[]{:S(2)}, u32[]{:S(2)}) %all-to-all-start.2) | async-done | bytes 786464 | tf_op jit(solution)/shard_map/all_to_all | solution.py:398
  142.1 7.1 %project_theirs.1 = bf16[128,3072]{1,0:T(8,128)(2,1)S(1)} custom-call(s32[1]{0:T(128)} %bitcast.6.which_ref, bf16[16,192,128]{2,1,0:T(8,128)(2,1)S(1)} %all-to-all-done.2.attended_ref, bf16[3072,6144]{1,0:T(8,128)(2,1)} %w_ref.3), custom_call_target="tpu_custom_call" | custom-call | flops 2415919104 | bytes 18874368 | tf_op jit(solution)/shard_map/project_theirs/pallas_call | solution.py:307
  149.2 0.1 collective-permute-start.2
  149.3 0.0 copy-start.2
  149.3 7.1 %project_mine.1 = f32[128,3072]{1,0:T(8,128)S(1)} custom-call(s32[1]{0:T(128)} %bitcast.which_ref, bf16[16,192,128]{2,1,0:T(8,128)(2,1)S(1)} %all-to-all-done.2.attended_ref, bf16[3072,6144]{1,0:T(8,128)(2,1)} %w_ref.3), custom_call_target="tpu_custom_call" | custom-call | flops 2415919104 | bytes 18874368 | tf_op jit(solution)/shard_map/project_mine/pallas_call | solution.py:307
  156.4 0.0 collective-permute-done.2
  156.4 0.0 copy-done.2
  156.4 1.1 multiply_convert_fusion
  (5 shorter events, 0.1 us)
Async XLA Ops:
  3.2 37.9 %all-to-all-start.1 = ((bf16[16,320,128]{2,1,0:T(8,128)(2,1)}), bf16[16,320,128]{2,1,0:T(8,128)(2,1)}, u32[]{:S(2)}, u32[]{:S(2)}) async-start(bf16[16,320,128]{2,1,0:T(8,128)(2,1)} %pack_shared.1), calls=%async_computation.1 | async-start | bytes 2621440 | tf_op jit(solution)/shard_map/all_to_all | solution.py:355
  15.4 32.5 %copy-start.4 = (s32[64]{0:T(128)S(1)}, s32[64]{0:T(128)}, u32[]{:S(2)}) copy-start(s32[64]{0:T(128)} %param.14) | copy-start | bytes 772
  15.4 32.6 %copy-start.3 = (s32[16,16]{1,0:T(8,128)S(1)}, s32[16,16]{1,0:T(8,128)}, u32[]{:S(2)}) copy-start(s32[16,16]{1,0:T(8,128)} %param.15) | copy-start | bytes 3076
  41.1 57.8 %all-to-all-start = ((bf16[16,640,128]{2,1,0:T(8,128)(2,1)}), bf16[16,640,128]{2,1,0:T(8,128)(2,1)S(1)}, u32[]{:S(2)}, u32[]{:S(2)}) async-start(bf16[16,640,128]{2,1,0:T(8,128)(2,1)} %pack_own.1), calls=%async_computation | async-start | bytes 5242880 | tf_op jit(solution)/shard_map/all_to_all | solution.py:356
  50.4 11.3 %collective-permute-start = (bf16[16,64,128]{2,1,0:T(8,128)(2,1)}, bf16[16,64,128]{2,1,0:T(8,128)(2,1)S(1)}, u32[]{:S(2)}, u32[]{:S(2)}) collective-permute-start(bf16[16,64,128]{2,1,0:T(8,128)(2,1)} %slice.49), channel_id=1, source_target_pairs={{0,2},{2,0},{4,6},{6,4},{8,10},{10,8},{12,14},{14,12},{16,18},{18,... | collective-permute-start | bytes 786440 | tf_op jit(solution)/shard_map/ppermute | solution.py:393
  66.6 25.8 %collective-permute-start.1 = (f32[4,136,256]{2,1,0:T(8,128)S(1)}, f32[4,136,256]{2,1,0:T(8,128)S(1)}, u32[]{:S(2)}, u32[]{:S(2)}) collective-permute-start(f32[4,136,256]{2,1,0:T(8,128)S(1)} %attend_theirs.1), channel_id=1, source_target_pairs={{0,2},{2,0},{4,6},{6,4},{8,10},{10,8},{12,14},{14,12},{16,18},{18,... | collective-permute-start | bytes 1671176 | tf_op jit(solution)/shard_map/ppermute | solution.py:396
  72.2 0.8 copy-start
  98.9 1.1 copy-start.1
  111.1 31.0 %all-to-all-start.2 = ((bf16[16,192,128]{2,1,0:T(8,128)(2,1)}), bf16[16,192,128]{2,1,0:T(8,128)(2,1)S(1)}, u32[]{:S(2)}, u32[]{:S(2)}) async-start(bf16[16,192,128]{2,1,0:T(8,128)(2,1)} %attend_own.1), calls=%async_computation.2 | async-start | bytes 1572864 | tf_op jit(solution)/shard_map/all_to_all | solution.py:398
  149.2 7.2 %collective-permute-start.2 = (bf16[128,3072]{1,0:T(8,128)(2,1)S(1)}, bf16[128,3072]{1,0:T(8,128)(2,1)S(1)}, u32[]{:S(2)}, u32[]{:S(2)}) collective-permute-start(bf16[128,3072]{1,0:T(8,128)(2,1)S(1)} %project_theirs.1), channel_id=1, source_target_pairs={{0,1},{1,0},{2,3},{3,2},{4,5},{5,4},{6,7},{7,6},{8,9},{9,8},{10,11... | collective-permute-start | bytes 2359304 | tf_op jit(solution)/shard_map/ppermute | solution.py:405
  149.3 7.1 %copy-start.2 = (f32[3072]{0:T(1024)S(1)}, f32[3072]{0:T(1024)}, u32[]{:S(2)}) copy-start(f32[3072]{0:T(1024)} %param.17) | copy-start | bytes 36868

commit v3 on v2

--- a/solution.py
+++ b/solution.py
@@ -107,15 +107,18 @@
     return (gate[None, :] * summed).astype(jnp.bfloat16)
 
 
-def pack_kernel(whole, *refs):
+def pack_kernel(pieces, *refs):
     n = (len(refs) - 2) // 2
     in_refs, out_ref, held, sems = refs[:n], refs[n], refs[n + 1 : -1], refs[-1]
     copies = [pltpu.make_async_copy(x, y, sems.at[i]) for i, (x, y) in enumerate(zip(in_refs, held))]
     for copy in copies:
         copy.start()
+    waiting = dict(enumerate(copies))
     at = 0
-    for copy, ref in zip(copies, held):
-        copy.wait()
+    for i, whole in pieces:
+        ref = held[i]
+        if i in waiting:
+            waiting.pop(i).wait()
         rows = ref.shape[0]
         half = rows // 2
         for j in range(ref.shape[1] // (3 * HD)):
@@ -131,12 +134,11 @@
         at += rows if whole else half
 
 
-def pack(arrays, whole, name):
+def pack(arrays, pieces, name):
     groups = arrays[0].shape[1] // (3 * HD)
-    rows = [x.shape[0] for x in arrays]
-    total = sum(rows) if whole else sum(rows) // 2
+    total = sum(arrays[i].shape[0] // (1 if whole else 2) for i, whole in pieces)
     return pl.pallas_call(
-        functools.partial(pack_kernel, whole),
+        functools.partial(pack_kernel, pieces),
         in_specs=[pl.BlockSpec(memory_space=pl.ANY) for _ in arrays],
         out_specs=pl.BlockSpec(memory_space=pltpu.VMEM),
         out_shape=jax.ShapeDtypeStruct((2 * groups, total, HD), arrays[0].dtype),
@@ -150,16 +152,26 @@
     )(*arrays)
 
 
-def attend_kernel(q_rows, keys_at, scale, carried, *refs):
+def join(one, numer, total_log):
+    one_log = one[HD : HD + 1, :]
+    top = jnp.maximum(one_log, total_log)
+    one_part, part = jnp.exp2(one_log - top), jnp.exp2(total_log - top)
+    joined = (one_part * one[:HD, :] + part * numer) / (one_part + part)
+    return joined.T.astype(jnp.bfloat16)
+
+
+def attend_kernel(q_from, q_rows, keys_at, scale, carried, *refs):
+    q_ref, kv_ref, bias_ref = refs[:3]
     if carried:
-        q_ref, kv_ref, bias_ref, mine_ref, theirs_ref, out_ref, k_all, v_all, kept_a, kept_b = refs
+        early_ref, out_ref, k_all, v_all, kept_a, kept_b, early, sem = refs[3:]
+        copy = pltpu.make_async_copy(early_ref, early, sem)
+        copy.start()
     else:
-        q_ref, kv_ref, bias_ref, out_ref, k_all, v_all, kept_a, kept_b = refs
+        out_ref, k_all, v_all, kept_a, kept_b = refs[3:]
     keys = k_all.shape[0]
     chips = TILE_ROWS // q_rows
     runs = TILE_ROWS // BLOCK
     tiles = q_ref.shape[0] // chips
-    half = q_rows // 2
 
     k_lo, k_hi, v_lo, v_hi = keys_at
     count = kv_ref.shape[0]
@@ -178,24 +190,18 @@
         total = jnp.sum(total, axis=0, keepdims=True)
         numer = numer / total
         tile = 2 * pair + odd
-        if not carried:
+        total_log = peak + jnp.log2(total)
+        if carried:
+            skip = out_ref.shape[1] - q_rows
+            joined = join(early[tile], numer, total_log)
+            out_ref[pl.ds(tile * chips, chips), skip:, :] = joined.reshape(chips, q_rows, HD)
+        else:
             out_ref[tile, :HD, :] = numer
-            out_ref[tile, HD:, :] = jnp.broadcast_to(peak + jnp.log2(total), (8, TILE_ROWS))
-            return
-        side = TILE_ROWS // 2
-        mine = mine_ref[pair, :, odd * side : (odd + 1) * side]
-        theirs = theirs_ref[pair, :, odd * side : (odd + 1) * side]
-        mine_log, their_log = mine[HD : HD + 1, :], theirs[HD : HD + 1, :]
-        top = jnp.maximum(mine_log, their_log)
-        mine_part, their_part = jnp.exp2(mine_log - top), jnp.exp2(their_log - top)
-        joined = (mine_part * mine[:HD, :] + their_part * theirs[:HD, :]) / (mine_part + their_part)
-        here = pl.ds(tile * chips, chips)
-        out_ref[here, :half, :] = joined.T.astype(out_ref.dtype).reshape(chips, half, HD)
-        out_ref[here, half:, :] = numer.T.astype(out_ref.dtype).reshape(chips, q_rows, HD)
+            out_ref[tile, HD:, :] = jnp.broadcast_to(total_log, (8, TILE_ROWS))
 
     def advance(ahead, ahead_kept, pair, odd, peak, kept):
         if ahead is not None:
-            q = q_ref[pl.ds(ahead * chips, chips), :q_rows, :].reshape(TILE_ROWS, HD).T
+            q = q_ref[pl.ds(ahead * chips, chips), q_from : q_from + q_rows, :].reshape(TILE_ROWS, HD).T
             row = lax.broadcasted_iota(jnp.int32, (HD, TILE_ROWS), 0)
             col = lax.broadcasted_iota(jnp.int32, (HD, TILE_ROWS), 1)
             run = (row == ahead * runs + col // BLOCK).astype(jnp.float32).astype(jnp.bfloat16)
@@ -225,6 +231,8 @@
             return jnp.max(new_peak, axis=0, keepdims=True) * scale
 
     peak = advance(0, kept_a, None, None, None, None)
+    if carried:
+        copy.wait()
 
     def two(pair, peak):
         peak = advance(2 * pair + 1, kept_b, pair, 0, peak, kept_a)
@@ -236,34 +244,73 @@
     advance(None, None, last, 1, peak, kept_b)
 
 
-def attend(q, q_rows, kv, keys_at, bias, carried, name):
+def attend(q, q_from, q_rows, kv, keys_at, bias, carried, spare, name):
     count = q.shape[0]
     chips = TILE_ROWS // q_rows
     keys = count * (keys_at[1] - keys_at[0])
     scale = math.log2(math.e) / math.sqrt(HD)
     work = count * q_rows * keys
+    vmem = pl.BlockSpec(memory_space=pltpu.VMEM)
+    in_specs = [vmem] * 3
+    scratch = [
+        pltpu.VMEM((keys, 2 * HD), jnp.bfloat16),
+        pltpu.VMEM((HD, keys), jnp.bfloat16),
+        pltpu.VMEM((keys, TILE_ROWS), jnp.float32),
+        pltpu.VMEM((keys, TILE_ROWS), jnp.float32),
+    ]
     if carried:
-        out_shape = jax.ShapeDtypeStruct((count, q_rows + q_rows // 2, HD), jnp.bfloat16)
+        in_specs += [pl.BlockSpec(memory_space=pl.ANY)]
+        scratch += [pltpu.VMEM(carried[0].shape, carried[0].dtype), pltpu.SemaphoreType.DMA(())]
+        carried = [pltpu.with_memory_space_constraint(x, pltpu.HBM) for x in carried]
+        out_shape = pltpu.HBM((count, spare + q_rows, HD), jnp.bfloat16)
     else:
-        out_shape = jax.ShapeDtypeStruct((count // chips, HD + 8, TILE_ROWS), jnp.float32)
-    vmem = pl.BlockSpec(memory_space=pltpu.VMEM)
+        out_shape = pltpu.HBM((count // chips, HD + 8, TILE_ROWS), jnp.float32)
     return pl.pallas_call(
-        functools.partial(attend_kernel, q_rows, keys_at, scale, bool(carried)),
-        in_specs=[vmem] * (3 + len(carried)),
+        functools.partial(attend_kernel, q_from, q_rows, keys_at, scale, bool(carried)),
+        in_specs=in_specs,
         out_specs=vmem,
         out_shape=out_shape,
-        scratch_shapes=[
-            pltpu.VMEM((keys, 2 * HD), jnp.bfloat16),
-            pltpu.VMEM((HD, keys), jnp.bfloat16),
-            pltpu.VMEM((keys, TILE_ROWS), jnp.float32),
-            pltpu.VMEM((keys, TILE_ROWS), jnp.float32),
-        ],
+        scratch_shapes=scratch,
         cost_estimate=pl.CostEstimate(
             flops=8 * work * HD, bytes_accessed=4 * 1024 * 1024, transcendentals=work
         ),
         compiler_params=pltpu.CompilerParams(vmem_limit_bytes=VMEM_LIMIT),
         name=name,
     )(q, kv, bias, *carried)
+
+
+def join_kernel(mine_ref, theirs_ref, whole_ref, out_ref, joined, sem):
+    del whole_ref
+    tiles = mine_ref.shape[0]
+    chips, rows = joined.shape[0] // tiles, joined.shape[1]
+    for tile in range(tiles):
+        theirs = theirs_ref[tile]
+        joined[tile * chips : (tile + 1) * chips] = join(
+            mine_ref[tile], theirs[:HD, :], theirs[HD : HD + 1, :]
+        ).reshape(chips, rows, HD)
+    copy = pltpu.make_async_copy(joined, out_ref.at[:, :rows, :], sem)
+    copy.start()
+    copy.wait()
+
+
+def join_shared(mine, theirs, attended, rows):
+    vmem = pl.BlockSpec(memory_space=pltpu.VMEM)
+    return pl.pallas_call(
+        join_kernel,
+        in_specs=[vmem, vmem, pl.BlockSpec(memory_space=pl.ANY)],
+        out_specs=pl.BlockSpec(memory_space=pl.ANY),
+        out_shape=jax.ShapeDtypeStruct(attended.shape, attended.dtype),
+        input_output_aliases={2: 0},
+        scratch_shapes=[
+            pltpu.VMEM((attended.shape[0], rows, HD), attended.dtype),
+            pltpu.SemaphoreType.DMA(()),
+        ],
+        cost_estimate=pl.CostEstimate(
+            flops=1 << 29, bytes_accessed=8 * mine.size, transcendentals=0
+        ),
+        compiler_params=pltpu.CompilerParams(vmem_limit_bytes=VMEM_LIMIT),
+        name="join_shared",
+    )(mine, theirs, pltpu.with_memory_space_constraint(attended, pltpu.HBM))
 
 
 def project_kernel(half, which_ref, attended_ref, w_ref, out_ref, left, held, acc, sems):
@@ -352,8 +399,10 @@
         pltpu.with_memory_space_constraint(x, pltpu.HBM)
         for x in (queries, context_keys, window_keys, context_values, window_values)
     ]
-    shared = lax.all_to_all(pack(arrays, False, "pack_shared"), "tm", 0, 0, tiled=True)
-    own = lax.all_to_all(pack(arrays, True, "pack_own"), "tm", 0, 0, tiled=True)
+    first = pack(arrays, [(i, False) for i in range(5)] + [(0, True), (1, True), (3, True)], "pack_first")
+    first = lax.all_to_all(first, "tm", 0, 0, tiled=True)
+    second = pack([arrays[2], arrays[4]], [(0, True), (1, True)], "pack_second")
+    second = lax.all_to_all(second, "tm", 0, 0, tiled=True)
 
     table = sees.astype(jnp.float32)
     groups = jnp.arange(sees.shape[0], dtype=jnp.int32)
@@ -370,7 +419,9 @@
         axis=1,
     )
     pad = lambda x: jnp.pad(x, ((0, 0), (0, HD - x.shape[1])))
-    own_bias = pad(bias.reshape(-1, n_query_blocks))
+    near_end = ctx_rows // BLOCK
+    ctx_bias = pad(bias[:, :near_end].reshape(-1, n_query_blocks))
+    win_bias = pad(bias[:, near_end:].reshape(-1, n_query_blocks))
     c_blocks, q_blocks = half_c // BLOCK, half_q // BLOCK
     near = jnp.where(
         side == 0,
@@ -387,14 +438,21 @@
     their_bias = jnp.where(side == 0, hi, lo)
 
     swap = [(i, i ^ 1) for i in range(tm_count)]
-    half_kv, full_kv = half_c + half_q, ctx_rows + tok_rows
+    half_kv = half_c + half_q
     shared_at = (half_q, half_q + half_kv, half_q + half_kv, half_q + 2 * half_kv)
-    own_at = (tok_rows, tok_rows + full_kv, tok_rows + full_kv, tok_rows + 2 * full_kv)
-    their_q = lax.ppermute(shared[:, :half_q, :], "tm", swap)
-    mine = attend(shared, half_q, shared, shared_at, my_bias, (), "attend_mine")
-    theirs = attend(their_q, half_q, shared, shared_at, their_bias, (), "attend_theirs")
+    own_q = half_q + 2 * half_kv
+    own_k = own_q + tok_rows
+    ctx_at = (own_k, own_k + ctx_rows, own_k + ctx_rows, own_k + 2 * ctx_rows)
+    win_at = (0, tok_rows, tok_rows, 2 * tok_rows)
+    their_q = lax.ppermute(first[:, :half_q, :], "tm", swap)
+    mine = attend(first, 0, half_q, first, shared_at, my_bias, (), 0, "attend_mine")
+    theirs = attend(their_q, 0, half_q, first, shared_at, their_bias, (), 0, "attend_theirs")
     theirs = lax.ppermute(theirs, "tm", swap)
-    attended = attend(own, tok_rows, own, own_at, own_bias, (mine, theirs), "attend_own")
+    early = attend(first, own_q, tok_rows, first, ctx_at, ctx_bias, (), 0, "attend_context")
+    attended = attend(
+        first, own_q, tok_rows, second, win_at, win_bias, (early,), half_q, "attend_window"
+    )
+    attended = join_shared(mine, theirs, attended, half_q)
     attended = lax.all_to_all(attended, "tm", 0, 0, tiled=True)
 
     columns = gate.shape[0]

time: 158 us -> 157 us (level)
  Pallas kernels: 42.5 us -> 46.9 us
  local copies, waits for them, and re-layouts: 6.26 us -> 2.54 us
  waiting for transfers between devices: 77.6 us -> 74.3 us
  starting transfers between devices: 29.5 us -> 31.3 us
    all_to_all x2, waiting for transfers between devices: 32.3 us -> 53.8 us  [the longest x1 53.8 us: dealt_body(): first = lax.all_to_all(first, 'tm', 0, 0, tiled=True)]
    ppermute x1, waiting for transfers between devices: 19.3 us -> 0.01 us  [dealt_body(): theirs = lax.ppermute(theirs, 'tm', swap)]
    all_to_all x1, starting transfers between devices: 12 us -> 4.83 us  [dealt_body(): attended = lax.all_to_all(attended, 'tm', 0, 0, tiled=True)]
    all_to_all x2, starting transfers between devices: 15.2 us -> 22.3 us  [the longest x1 13.9 us: dealt_body(): second = lax.all_to_all(second, 'tm', 0, 0, tiled=True)]
    ppermute x1, waiting for transfers between devices: 7.06 us -> 1.82 us  [dealt_body(): their_q = lax.ppermute(first[:, :half_q, :], 'tm', swap)]
    pallas_call x5 -> x7, Pallas kernels: 28.3 us -> 32.7 us  [the longest x4 25.4 us: attend(): pl.pallas_call(functools.partial(attend_kernel, q_from, q_rows, keys_at,...]
    ppermute x1, starting transfers between devices: 0.32 us -> 2.2 us  [dealt_body(): theirs = lax.ppermute(theirs, 'tm', swap)]
    unnamed x12 -> x10, local copies, waits for them, and re-layouts: 3.31 us -> 1.46 us
  transfers between devices with their start and end apart: 6 -> 6, of which waited for: 5 -> 3; matrix products, arithmetic and copies ran while one was open for 3% -> 2% of each run, Pallas kernels for 13% -> 22%
where the time goes in v3:
time: 157 us
  waiting for transfers between devices  74.3 us (47%)
  Pallas kernels  46.9 us (30%)
  starting transfers between devices  31.3 us (20%)
  local copies, waits for them, and re-layouts  2.54 us (2%)
    all_to_all x1, waiting for transfers between devices, dealt_body(): first = lax.all_to_all(first, 'tm', 0, 0, tiled=True)  53.8 us
    pallas_call x4, Pallas kernels, attend(): pl.pallas_call(functools.partial(attend_kernel, q_from, q_rows, keys_at,...  25.4 us
    all_to_all x1, waiting for transfers between devices, dealt_body(): attended = lax.all_to_all(attended, 'tm', 0, 0, tiled=True)  18.7 us
    pallas_call x2, Pallas kernels, project(): pl.pallas_call(functools.partial(project_kernel, half), in_specs=[pl.Bloc...  14.2 us
    all_to_all x1, starting transfers between devices, dealt_body(): second = lax.all_to_all(second, 'tm', 0, 0, tiled=True)  13.9 us
    all_to_all x1, starting transfers between devices, dealt_body(): first = lax.all_to_all(first, 'tm', 0, 0, tiled=True)  8.35 us
    pallas_call x2, Pallas kernels, pack(): pl.pallas_call(functools.partial(pack_kernel, pieces), in_specs=[pl.Block...  6.44 us
    all_to_all x1, starting transfers between devices, dealt_body(): attended = lax.all_to_all(attended, 'tm', 0, 0, tiled=True)  4.83 us
  transfers between devices with their start and end apart: 6, of which 3 were waited for; matrix products, arithmetic and copies ran while one was open for 2% of the time, Pallas kernels for 22%

profile of v3, /device:TPU:0, one launch (start us, length us, event | category | flops | bytes accessed | tf_op | source)
XLA Modules:
  0.0 156.8 jit_solution(16899448615111978916)
XLA Ops:
  0.0 4.0 %pack_first.1 = bf16[16,704,128]{2,1,0:T(8,128)(2,1)} custom-call(bf16[128,3072]{1,0:T(8,128)(2,1)} %refs_0_.2, bf16[128,3072]{1,0:T(8,128)(2,1)} %refs_1_.2, bf16[128,3072]{1,0:T(8,128)(2,1)} %refs_0_.3, bf16[128,3072]{1,0:T(8,128)(2,1)} %refs_3_.1, bf16[128,3072]{1,0:T(8,128)(2,1)} %refs_1_.3), custom_call_target="tpu_custom_call" | custom-call | flops 536870912 | bytes 8388608 | tf_op jit(solution)/shard_map/pack_first/pallas_call | solution.py:140
  4.0 8.4 %all-to-all-start = ((bf16[16,704,128]{2,1,0:T(8,128)(2,1)}), bf16[16,704,128]{2,1,0:T(8,128)(2,1)S(1)}, u32[]{:S(2)}, u32[]{:S(2)}) async-start(bf16[16,704,128]{2,1,0:T(8,128)(2,1)} %pack_first.1), calls=%async_computation | async-start | bytes 5767168 | tf_op jit(solution)/shard_map/all_to_all | solution.py:403
  12.4 2.5 %pack_second.1 = bf16[16,256,128]{2,1,0:T(8,128)(2,1)} custom-call(bf16[128,3072]{1,0:T(8,128)(2,1)} %refs_0_.3, bf16[128,3072]{1,0:T(8,128)(2,1)} %refs_1_.3), custom_call_target="tpu_custom_call" | custom-call | flops 536870912 | bytes 8388608 | tf_op jit(solution)/shard_map/pack_second/pallas_call | solution.py:140
  14.8 0.0 copy-start.3
  14.8 0.0 copy-start.2
  14.8 53.8 %all-to-all-done.refs_0_.refs_1_ = bf16[16,704,128]{2,1,0:T(8,128)(2,1)S(1)} async-done(((bf16[16,704,128]{2,1,0:T(8,128)(2,1)}), bf16[16,704,128]{2,1,0:T(8,128)(2,1)S(1)}, u32[]{:S(2)}, u32[]{:S(2)}) %all-to-all-start) | async-done | bytes 2883616 | tf_op jit(solution)/shard_map/all_to_all | solution.py:403
  68.7 13.9 %all-to-all-start.1 = ((bf16[16,256,128]{2,1,0:T(8,128)(2,1)}), bf16[16,256,128]{2,1,0:T(8,128)(2,1)}, u32[]{:S(2)}, u32[]{:S(2)}) async-start(bf16[16,256,128]{2,1,0:T(8,128)(2,1)} %pack_second.1), calls=%async_computation.1 | async-start | bytes 2097152 | tf_op jit(solution)/shard_map/all_to_all | solution.py:405
  82.6 0.0 copy-done.3
  82.6 0.1 iota_compare_fusion
  82.7 0.0 copy-done.2
  82.7 0.2 fusion.6
  83.0 0.2 select_n.46
  83.2 0.8 fusion.12
  84.1 1.2 copy.17
  85.2 0.3 copy.16
  85.6 1.9 %collective-permute-start = (bf16[16,64,128]{2,1,0:T(8,128)(2,1)S(1)}, bf16[16,64,128]{2,1,0:T(8,128)(2,1)S(1)}, u32[]{:S(2)}, u32[]{:S(2)}) collective-permute-start(bf16[16,64,128]{2,1,0:T(8,128)(2,1)S(1)} %slice.49), channel_id=1, source_target_pairs={{0,2},{2,0},{4,6},{6,4},{8,10},{10,8},{12,14},{14,12},{16,18},{18,... | collective-permute-start | bytes 786440 | tf_op jit(solution)/shard_map/ppermute | solution.py:447
  87.5 7.5 %attend_context.1.refs_3_ = f32[8,136,256]{2,1,0:T(8,128)} custom-call(bf16[16,704,128]{2,1,0:T(8,128)(2,1)S(1)} %all-to-all-done.refs_0_.refs_1_, bf16[16,704,128]{2,1,0:T(8,128)(2,1)S(1)} %all-to-all-done.refs_0_.refs_1_, f32[32,128]{1,0:T(8,128)S(1)} %pad.17.refs_2_), custom_call_target="tpu_custom_call" | custom-call | flops 4294967296 | bytes 4194304 | tf_op jit(solution)/shard_map/attend_context/pallas_call | solution.py:268
  95.0 1.8 %collective-permute-done.refs_0_ = bf16[16,64,128]{2,1,0:T(8,128)(2,1)S(1)} collective-permute-done((bf16[16,64,128]{2,1,0:T(8,128)(2,1)S(1)}, bf16[16,64,128]{2,1,0:T(8,128)(2,1)S(1)}, u32[]{:S(2)}, u32[]{:S(2)}) %collective-permute-start) | collective-permute-done | bytes 262176 | tf_op jit(solution)/shard_map/ppermute | solution.py:447
  96.8 4.4 %attend_theirs.1 = f32[4,136,256]{2,1,0:T(8,128)} custom-call(bf16[16,64,128]{2,1,0:T(8,128)(2,1)S(1)} %collective-permute-done.refs_0_, bf16[16,704,128]{2,1,0:T(8,128)(2,1)S(1)} %all-to-all-done.refs_0_.refs_1_, f32[32,128]{1,0:T(8,128)S(1)} %get-tuple-element.7.refs_2_), custom_call_target="tpu_custom_call" | custom-call | flops 2147483648 | bytes 4194304 | tf_op jit(solution)/shard_map/attend_theirs/pallas_call | solution.py:268
  101.2 2.2 %collective-permute-start.1 = (f32[4,136,256]{2,1,0:T(8,128)}, f32[4,136,256]{2,1,0:T(8,128)S(1)}, u32[]{:S(2)}, u32[]{:S(2)}) collective-permute-start(f32[4,136,256]{2,1,0:T(8,128)} %attend_theirs.1), channel_id=1, source_target_pairs={{0,2},{2,0},{4,6},{6,4},{8,10},{10,8},{12,14},{14,12},{16,18},{18,... | collective-permute-start | bytes 1671176 | tf_op jit(solution)/shard_map/ppermute | solution.py:450
  103.4 4.4 %attend_mine.1.mine_ref = f32[4,136,256]{2,1,0:T(8,128)} custom-call(bf16[16,704,128]{2,1,0:T(8,128)(2,1)S(1)} %all-to-all-done.refs_0_.refs_1_, bf16[16,704,128]{2,1,0:T(8,128)(2,1)S(1)} %all-to-all-done.refs_0_.refs_1_, f32[32,128]{1,0:T(8,128)S(1)} %get-tuple-element.8.refs_2_), custom_call_target="tpu_custom_call" | custom-call | flops 2147483648 | bytes 4194304 | tf_op jit(solution)/shard_map/attend_mine/pallas_call | solution.py:268
  107.8 0.0 all-to-all-done.1.refs_1_
  107.8 0.0 copy-start
  107.8 9.1 %attend_window.1.whole_ref = bf16[16,192,128]{2,1,0:T(8,128)(2,1)} custom-call(bf16[16,704,128]{2,1,0:T(8,128)(2,1)S(1)} %all-to-all-done.refs_0_.refs_1_, bf16[16,256,128]{2,1,0:T(8,128)(2,1)} %all-to-all-done.1.refs_1_, f32[32,128]{1,0:T(8,128)S(1)} %pad.16.refs_2_, f32[8,136,256]{2,1,0:T(8,128)} %attend_context.1.refs_3_), custom_call_target="tpu_custom_call" | custom-call | flops 4294967296 | bytes 4194304 | tf_op jit(solution)/shard_map/attend_window/pallas_call | solution.py:268
  116.9 0.0 collective-permute-done.1.theirs_ref
  116.9 0.0 copy-done
  116.9 0.9 join_shared.1
  117.8 4.8 %all-to-all-start.2 = ((bf16[16,192,128]{2,1,0:T(8,128)(2,1)}), bf16[16,192,128]{2,1,0:T(8,128)(2,1)S(1)}, u32[]{:S(2)}, u32[]{:S(2)}) async-start(bf16[16,192,128]{2,1,0:T(8,128)(2,1)} %join_shared.1), calls=%async_computation.2 | async-start | bytes 1572864 | tf_op jit(solution)/shard_map/all_to_all | solution.py:456
  122.7 18.7 %all-to-all-done.2.attended_ref = bf16[16,192,128]{2,1,0:T(8,128)(2,1)S(1)} async-done(((bf16[16,192,128]{2,1,0:T(8,128)(2,1)}), bf16[16,192,128]{2,1,0:T(8,128)(2,1)S(1)}, u32[]{:S(2)}, u32[]{:S(2)}) %all-to-all-start.2) | async-done | bytes 786464 | tf_op jit(solution)/shard_map/all_to_all | solution.py:456
  141.4 7.1 %project_theirs.1 = bf16[128,3072]{1,0:T(8,128)(2,1)S(1)} custom-call(s32[1]{0:T(128)} %bitcast.5.which_ref, bf16[16,192,128]{2,1,0:T(8,128)(2,1)S(1)} %all-to-all-done.2.attended_ref, bf16[3072,6144]{1,0:T(8,128)(2,1)} %w_ref.3), custom_call_target="tpu_custom_call" | custom-call | flops 2415919104 | bytes 18874368 | tf_op jit(solution)/shard_map/project_theirs/pallas_call | solution.py:354
  148.5 0.1 collective-permute-start.2
  148.5 0.0 copy-start.1
  148.5 7.1 %project_mine.1 = f32[128,3072]{1,0:T(8,128)S(1)} custom-call(s32[1]{0:T(128)} %bitcast.which_ref, bf16[16,192,128]{2,1,0:T(8,128)(2,1)S(1)} %all-to-all-done.2.attended_ref, bf16[3072,6144]{1,0:T(8,128)(2,1)} %w_ref.3), custom_call_target="tpu_custom_call" | custom-call | flops 2415919104 | bytes 18874368 | tf_op jit(solution)/shard_map/project_mine/pallas_call | solution.py:354
  155.6 0.0 collective-permute-done.2
  155.7 0.0 copy-done.1
  155.7 1.1 multiply_convert_fusion
  (7 shorter events, 0.1 us)
Async XLA Ops:
  4.0 64.7 %all-to-all-start = ((bf16[16,704,128]{2,1,0:T(8,128)(2,1)}), bf16[16,704,128]{2,1,0:T(8,128)(2,1)S(1)}, u32[]{:S(2)}, u32[]{:S(2)}) async-start(bf16[16,704,128]{2,1,0:T(8,128)(2,1)} %pack_first.1), calls=%async_computation | async-start | bytes 5767168 | tf_op jit(solution)/shard_map/all_to_all | solution.py:403
  14.8 67.8 %copy-start.3 = (s32[64]{0:T(128)S(1)}, s32[64]{0:T(128)}, u32[]{:S(2)}) copy-start(s32[64]{0:T(128)} %param.14) | copy-start | bytes 772
  14.8 67.9 %copy-start.2 = (s32[16,16]{1,0:T(8,128)S(1)}, s32[16,16]{1,0:T(8,128)}, u32[]{:S(2)}) copy-start(s32[16,16]{1,0:T(8,128)} %param.15) | copy-start | bytes 3076
  68.7 39.1 %all-to-all-start.1 = ((bf16[16,256,128]{2,1,0:T(8,128)(2,1)}), bf16[16,256,128]{2,1,0:T(8,128)(2,1)}, u32[]{:S(2)}, u32[]{:S(2)}) async-start(bf16[16,256,128]{2,1,0:T(8,128)(2,1)} %pack_second.1), calls=%async_computation.1 | async-start | bytes 2097152 | tf_op jit(solution)/shard_map/all_to_all | solution.py:405
  85.6 11.3 %collective-permute-start = (bf16[16,64,128]{2,1,0:T(8,128)(2,1)S(1)}, bf16[16,64,128]{2,1,0:T(8,128)(2,1)S(1)}, u32[]{:S(2)}, u32[]{:S(2)}) collective-permute-start(bf16[16,64,128]{2,1,0:T(8,128)(2,1)S(1)} %slice.49), channel_id=1, source_target_pairs={{0,2},{2,0},{4,6},{6,4},{8,10},{10,8},{12,14},{14,12},{16,18},{18,... | collective-permute-start | bytes 786440 | tf_op jit(solution)/shard_map/ppermute | solution.py:447
  101.2 15.7 %collective-permute-start.1 = (f32[4,136,256]{2,1,0:T(8,128)}, f32[4,136,256]{2,1,0:T(8,128)S(1)}, u32[]{:S(2)}, u32[]{:S(2)}) collective-permute-start(f32[4,136,256]{2,1,0:T(8,128)} %attend_theirs.1), channel_id=1, source_target_pairs={{0,2},{2,0},{4,6},{6,4},{8,10},{10,8},{12,14},{14,12},{16,18},{18,... | collective-permute-start | bytes 1671176 | tf_op jit(solution)/shard_map/ppermute | solution.py:450
  107.8 9.1 %copy-start = (f32[4,136,256]{2,1,0:T(8,128)S(1)}, f32[4,136,256]{2,1,0:T(8,128)}, u32[]{:S(2)}) copy-start(f32[4,136,256]{2,1,0:T(8,128)} %attend_mine.1.mine_ref) | copy-start | bytes 1671172
  117.8 23.5 %all-to-all-start.2 = ((bf16[16,192,128]{2,1,0:T(8,128)(2,1)}), bf16[16,192,128]{2,1,0:T(8,128)(2,1)S(1)}, u32[]{:S(2)}, u32[]{:S(2)}) async-start(bf16[16,192,128]{2,1,0:T(8,128)(2,1)} %join_shared.1), calls=%async_computation.2 | async-start | bytes 1572864 | tf_op jit(solution)/shard_map/all_to_all | solution.py:456
  148.5 7.2 %collective-permute-start.2 = (bf16[128,3072]{1,0:T(8,128)(2,1)S(1)}, bf16[128,3072]{1,0:T(8,128)(2,1)S(1)}, u32[]{:S(2)}, u32[]{:S(2)}) collective-permute-start(bf16[128,3072]{1,0:T(8,128)(2,1)S(1)} %project_theirs.1), channel_id=1, source_target_pairs={{0,1},{1,0},{2,3},{3,2},{4,5},{5,4},{6,7},{7,6},{8,9},{9,8},{10,11... | collective-permute-start | bytes 2359304 | tf_op jit(solution)/shard_map/ppermute | solution.py:463
  148.5 7.1 %copy-start.1 = (f32[3072]{0:T(1024)S(1)}, f32[3072]{0:T(1024)}, u32[]{:S(2)}) copy-start(f32[3072]{0:T(1024)} %param.17) | copy-start | bytes 36868

commit v4 on v3

--- a/solution.py
+++ b/solution.py
@@ -108,8 +108,10 @@
 
 
 def pack_kernel(pieces, *refs):
-    n = (len(refs) - 2) // 2
-    in_refs, out_ref, held, sems = refs[:n], refs[n], refs[n + 1 : -1], refs[-1]
+    n = (len(refs) - 4) // 2
+    in_refs, result_ref, held = refs[:n], refs[n], refs[n + 1 : 2 * n + 1]
+    out_ref, sems, out_sems = refs[2 * n + 1 :]
+    leaving = []
     copies = [pltpu.make_async_copy(x, y, sems.at[i]) for i, (x, y) in enumerate(zip(in_refs, held))]
     for copy in copies:
         copy.start()
@@ -131,7 +133,16 @@
                     out_ref[2 * j + side, at : at + half, :] = ref[
                         side * half : (side + 1) * half, head * HD : (head + 1) * HD
                     ]
+        here = pl.ds(at, rows if whole else half)
+        leaving.append(
+            pltpu.make_async_copy(
+                out_ref.at[:, here, :], result_ref.at[:, here, :], out_sems.at[len(leaving)]
+            )
+        )
+        leaving[-1].start()
         at += rows if whole else half
+    for copy in leaving:
+        copy.wait()
 
 
 def pack(arrays, pieces, name):
@@ -140,10 +151,14 @@
     return pl.pallas_call(
         functools.partial(pack_kernel, pieces),
         in_specs=[pl.BlockSpec(memory_space=pl.ANY) for _ in arrays],
-        out_specs=pl.BlockSpec(memory_space=pltpu.VMEM),
-        out_shape=jax.ShapeDtypeStruct((2 * groups, total, HD), arrays[0].dtype),
+        out_specs=pl.BlockSpec(memory_space=pl.ANY),
+        out_shape=pltpu.HBM((2 * groups, total, HD), arrays[0].dtype),
         scratch_shapes=[pltpu.VMEM(x.shape, x.dtype) for x in arrays]
-        + [pltpu.SemaphoreType.DMA((len(arrays),))],
+        + [
+            pltpu.VMEM((2 * groups, total, HD), arrays[0].dtype),
+            pltpu.SemaphoreType.DMA((len(arrays),)),
+            pltpu.SemaphoreType.DMA((len(pieces),)),
+        ],
         cost_estimate=pl.CostEstimate(
             flops=1 << 29, bytes_accessed=8 * 1024 * 1024, transcendentals=0
         ),

time: 157 us -> 157 us (level)
  no operation moved by 1% of the time
where the time goes in v4:
time: 157 us; the launch traced here: 156 us
  waiting for transfers between devices  74.5 us (47%)
  Pallas kernels  46.3 us (29%)
  starting transfers between devices  31.3 us (20%)
  local copies, waits for them, and re-layouts  2.54 us (2%)
    all_to_all x1, waiting for transfers between devices, dealt_body(): first = lax.all_to_all(first, 'tm', 0, 0, tiled=True)  54 us
    pallas_call x4, Pallas kernels, attend(): pl.pallas_call(functools.partial(attend_kernel, q_from, q_rows, keys_at,...  25.4 us
    all_to_all x1, waiting for transfers between devices, dealt_body(): attended = lax.all_to_all(attended, 'tm', 0, 0, tiled=True)  18.7 us
    pallas_call x2, Pallas kernels, project(): pl.pallas_call(functools.partial(project_kernel, half), in_specs=[pl.Bloc...  14.2 us
    all_to_all x1, starting transfers between devices, dealt_body(): second = lax.all_to_all(second, 'tm', 0, 0, tiled=True)  13.9 us
    all_to_all x1, starting transfers between devices, dealt_body(): first = lax.all_to_all(first, 'tm', 0, 0, tiled=True)  8.35 us
    pallas_call x2, Pallas kernels, pack(): pl.pallas_call(functools.partial(pack_kernel, pieces), in_specs=[pl.Block...  5.83 us
    all_to_all x1, starting transfers between devices, dealt_body(): attended = lax.all_to_all(attended, 'tm', 0, 0, tiled=True)  4.84 us
  transfers between devices with their start and end apart: 6, of which 3 were waited for; matrix products, arithmetic and copies ran while one was open for 2% of the time, Pallas kernels for 22%

profile of v4, /device:TPU:0, one launch (start us, length us, event | category | flops | bytes accessed | tf_op | source)
XLA Modules:
  0.0 156.3 jit_solution(4122313628019998551)
XLA Ops:
  0.0 3.5 %pack_first.1 = bf16[16,704,128]{2,1,0:T(8,128)(2,1)} custom-call(bf16[128,3072]{1,0:T(8,128)(2,1)} %refs_0_.2, bf16[128,3072]{1,0:T(8,128)(2,1)} %refs_1_.2, bf16[128,3072]{1,0:T(8,128)(2,1)} %refs_0_.3, bf16[128,3072]{1,0:T(8,128)(2,1)} %refs_3_.1, bf16[128,3072]{1,0:T(8,128)(2,1)} %refs_1_.3), custom_call_target="tpu_custom_call" | custom-call | flops 536870912 | bytes 8388608 | tf_op jit(solution)/shard_map/pack_first/pallas_call | solution.py:151
  3.5 8.4 %all-to-all-start = ((bf16[16,704,128]{2,1,0:T(8,128)(2,1)}), bf16[16,704,128]{2,1,0:T(8,128)(2,1)S(1)}, u32[]{:S(2)}, u32[]{:S(2)}) async-start(bf16[16,704,128]{2,1,0:T(8,128)(2,1)} %pack_first.1), calls=%async_computation | async-start | bytes 5767168 | tf_op jit(solution)/shard_map/all_to_all | solution.py:418
  11.9 2.3 %pack_second.1 = bf16[16,256,128]{2,1,0:T(8,128)(2,1)} custom-call(bf16[128,3072]{1,0:T(8,128)(2,1)} %refs_0_.3, bf16[128,3072]{1,0:T(8,128)(2,1)} %refs_1_.3), custom_call_target="tpu_custom_call" | custom-call | flops 536870912 | bytes 8388608 | tf_op jit(solution)/shard_map/pack_second/pallas_call | solution.py:151
  14.2 0.0 copy-start.3
  14.2 0.0 copy-start.2
  14.2 54.0 %all-to-all-done.refs_0_.refs_1_ = bf16[16,704,128]{2,1,0:T(8,128)(2,1)S(1)} async-done(((bf16[16,704,128]{2,1,0:T(8,128)(2,1)}), bf16[16,704,128]{2,1,0:T(8,128)(2,1)S(1)}, u32[]{:S(2)}, u32[]{:S(2)}) %all-to-all-start) | async-done | bytes 2883616 | tf_op jit(solution)/shard_map/all_to_all | solution.py:418
  68.2 13.9 %all-to-all-start.1 = ((bf16[16,256,128]{2,1,0:T(8,128)(2,1)}), bf16[16,256,128]{2,1,0:T(8,128)(2,1)}, u32[]{:S(2)}, u32[]{:S(2)}) async-start(bf16[16,256,128]{2,1,0:T(8,128)(2,1)} %pack_second.1), calls=%async_computation.1 | async-start | bytes 2097152 | tf_op jit(solution)/shard_map/all_to_all | solution.py:420
  82.1 0.0 copy-done.3
  82.1 0.1 iota_compare_fusion
  82.2 0.0 copy-done.2
  82.2 0.2 fusion.6
  82.6 0.2 select_n.46
  82.8 0.8 fusion.12
  83.6 1.2 copy.17
  84.8 0.3 copy.16
  85.1 1.9 %collective-permute-start = (bf16[16,64,128]{2,1,0:T(8,128)(2,1)S(1)}, bf16[16,64,128]{2,1,0:T(8,128)(2,1)S(1)}, u32[]{:S(2)}, u32[]{:S(2)}) collective-permute-start(bf16[16,64,128]{2,1,0:T(8,128)(2,1)S(1)} %slice.49), channel_id=1, source_target_pairs={{0,2},{2,0},{4,6},{6,4},{8,10},{10,8},{12,14},{14,12},{16,18},{18,... | collective-permute-start | bytes 786440 | tf_op jit(solution)/shard_map/ppermute | solution.py:462
  87.0 7.5 %attend_context.1.refs_3_ = f32[8,136,256]{2,1,0:T(8,128)} custom-call(bf16[16,704,128]{2,1,0:T(8,128)(2,1)S(1)} %all-to-all-done.refs_0_.refs_1_, bf16[16,704,128]{2,1,0:T(8,128)(2,1)S(1)} %all-to-all-done.refs_0_.refs_1_, f32[32,128]{1,0:T(8,128)S(1)} %pad.17.refs_2_), custom_call_target="tpu_custom_call" | custom-call | flops 4294967296 | bytes 4194304 | tf_op jit(solution)/shard_map/attend_context/pallas_call | solution.py:283
  94.6 1.8 %collective-permute-done.refs_0_ = bf16[16,64,128]{2,1,0:T(8,128)(2,1)S(1)} collective-permute-done((bf16[16,64,128]{2,1,0:T(8,128)(2,1)S(1)}, bf16[16,64,128]{2,1,0:T(8,128)(2,1)S(1)}, u32[]{:S(2)}, u32[]{:S(2)}) %collective-permute-start) | collective-permute-done | bytes 262176 | tf_op jit(solution)/shard_map/ppermute | solution.py:462
  96.4 4.4 %attend_theirs.1 = f32[4,136,256]{2,1,0:T(8,128)} custom-call(bf16[16,64,128]{2,1,0:T(8,128)(2,1)S(1)} %collective-permute-done.refs_0_, bf16[16,704,128]{2,1,0:T(8,128)(2,1)S(1)} %all-to-all-done.refs_0_.refs_1_, f32[32,128]{1,0:T(8,128)S(1)} %get-tuple-element.7.refs_2_), custom_call_target="tpu_custom_call" | custom-call | flops 2147483648 | bytes 4194304 | tf_op jit(solution)/shard_map/attend_theirs/pallas_call | solution.py:283
  100.8 2.2 %collective-permute-start.1 = (f32[4,136,256]{2,1,0:T(8,128)}, f32[4,136,256]{2,1,0:T(8,128)S(1)}, u32[]{:S(2)}, u32[]{:S(2)}) collective-permute-start(f32[4,136,256]{2,1,0:T(8,128)} %attend_theirs.1), channel_id=1, source_target_pairs={{0,2},{2,0},{4,6},{6,4},{8,10},{10,8},{12,14},{14,12},{16,18},{18,... | collective-permute-start | bytes 1671176 | tf_op jit(solution)/shard_map/ppermute | solution.py:465
  103.0 4.4 %attend_mine.1.mine_ref = f32[4,136,256]{2,1,0:T(8,128)} custom-call(bf16[16,704,128]{2,1,0:T(8,128)(2,1)S(1)} %all-to-all-done.refs_0_.refs_1_, bf16[16,704,128]{2,1,0:T(8,128)(2,1)S(1)} %all-to-all-done.refs_0_.refs_1_, f32[32,128]{1,0:T(8,128)S(1)} %get-tuple-element.8.refs_2_), custom_call_target="tpu_custom_call" | custom-call | flops 2147483648 | bytes 4194304 | tf_op jit(solution)/shard_map/attend_mine/pallas_call | solution.py:283
  107.3 0.0 all-to-all-done.1.refs_1_
  107.4 0.0 copy-start
  107.4 9.1 %attend_window.1.whole_ref = bf16[16,192,128]{2,1,0:T(8,128)(2,1)} custom-call(bf16[16,704,128]{2,1,0:T(8,128)(2,1)S(1)} %all-to-all-done.refs_0_.refs_1_, bf16[16,256,128]{2,1,0:T(8,128)(2,1)} %all-to-all-done.1.refs_1_, f32[32,128]{1,0:T(8,128)S(1)} %pad.16.refs_2_, f32[8,136,256]{2,1,0:T(8,128)} %attend_context.1.refs_3_), custom_call_target="tpu_custom_call" | custom-call | flops 4294967296 | bytes 4194304 | tf_op jit(solution)/shard_map/attend_window/pallas_call | solution.py:283
  116.4 0.0 collective-permute-done.1.theirs_ref
  116.5 0.0 copy-done
  116.5 0.9 join_shared.1
  117.4 4.8 %all-to-all-start.2 = ((bf16[16,192,128]{2,1,0:T(8,128)(2,1)}), bf16[16,192,128]{2,1,0:T(8,128)(2,1)S(1)}, u32[]{:S(2)}, u32[]{:S(2)}) async-start(bf16[16,192,128]{2,1,0:T(8,128)(2,1)} %join_shared.1), calls=%async_computation.2 | async-start | bytes 1572864 | tf_op jit(solution)/shard_map/all_to_all | solution.py:471
  122.2 18.7 %all-to-all-done.2.attended_ref = bf16[16,192,128]{2,1,0:T(8,128)(2,1)S(1)} async-done(((bf16[16,192,128]{2,1,0:T(8,128)(2,1)}), bf16[16,192,128]{2,1,0:T(8,128)(2,1)S(1)}, u32[]{:S(2)}, u32[]{:S(2)}) %all-to-all-start.2) | async-done | bytes 786464 | tf_op jit(solution)/shard_map/all_to_all | solution.py:471
  140.9 7.1 %project_theirs.1 = bf16[128,3072]{1,0:T(8,128)(2,1)S(1)} custom-call(s32[1]{0:T(128)} %bitcast.5.which_ref, bf16[16,192,128]{2,1,0:T(8,128)(2,1)S(1)} %all-to-all-done.2.attended_ref, bf16[3072,6144]{1,0:T(8,128)(2,1)} %w_ref.3), custom_call_target="tpu_custom_call" | custom-call | flops 2415919104 | bytes 18874368 | tf_op jit(solution)/shard_map/project_theirs/pallas_call | solution.py:369
  148.0 0.1 collective-permute-start.2
  148.1 0.0 copy-start.1
  148.1 7.1 %project_mine.1 = f32[128,3072]{1,0:T(8,128)S(1)} custom-call(s32[1]{0:T(128)} %bitcast.which_ref, bf16[16,192,128]{2,1,0:T(8,128)(2,1)S(1)} %all-to-all-done.2.attended_ref, bf16[3072,6144]{1,0:T(8,128)(2,1)} %w_ref.3), custom_call_target="tpu_custom_call" | custom-call | flops 2415919104 | bytes 18874368 | tf_op jit(solution)/shard_map/project_mine/pallas_call | solution.py:369
  155.2 0.0 collective-permute-done.2
  155.2 0.0 copy-done.1
  155.2 1.1 multiply_convert_fusion
  (7 shorter events, 0.1 us)
Async XLA Ops:
  3.5 64.7 %all-to-all-start = ((bf16[16,704,128]{2,1,0:T(8,128)(2,1)}), bf16[16,704,128]{2,1,0:T(8,128)(2,1)S(1)}, u32[]{:S(2)}, u32[]{:S(2)}) async-start(bf16[16,704,128]{2,1,0:T(8,128)(2,1)} %pack_first.1), calls=%async_computation | async-start | bytes 5767168 | tf_op jit(solution)/shard_map/all_to_all | solution.py:418
  14.2 67.9 %copy-start.3 = (s32[64]{0:T(128)S(1)}, s32[64]{0:T(128)}, u32[]{:S(2)}) copy-start(s32[64]{0:T(128)} %param.14) | copy-start | bytes 772
  14.2 68.0 %copy-start.2 = (s32[16,16]{1,0:T(8,128)S(1)}, s32[16,16]{1,0:T(8,128)}, u32[]{:S(2)}) copy-start(s32[16,16]{1,0:T(8,128)} %param.15) | copy-start | bytes 3076
  68.2 39.1 %all-to-all-start.1 = ((bf16[16,256,128]{2,1,0:T(8,128)(2,1)}), bf16[16,256,128]{2,1,0:T(8,128)(2,1)}, u32[]{:S(2)}, u32[]{:S(2)}) async-start(bf16[16,256,128]{2,1,0:T(8,128)(2,1)} %pack_second.1), calls=%async_computation.1 | async-start | bytes 2097152 | tf_op jit(solution)/shard_map/all_to_all | solution.py:420
  85.1 11.3 %collective-permute-start = (bf16[16,64,128]{2,1,0:T(8,128)(2,1)S(1)}, bf16[16,64,128]{2,1,0:T(8,128)(2,1)S(1)}, u32[]{:S(2)}, u32[]{:S(2)}) collective-permute-start(bf16[16,64,128]{2,1,0:T(8,128)(2,1)S(1)} %slice.49), channel_id=1, source_target_pairs={{0,2},{2,0},{4,6},{6,4},{8,10},{10,8},{12,14},{14,12},{16,18},{18,... | collective-permute-start | bytes 786440 | tf_op jit(solution)/shard_map/ppermute | solution.py:462
  100.8 15.7 %collective-permute-start.1 = (f32[4,136,256]{2,1,0:T(8,128)}, f32[4,136,256]{2,1,0:T(8,128)S(1)}, u32[]{:S(2)}, u32[]{:S(2)}) collective-permute-start(f32[4,136,256]{2,1,0:T(8,128)} %attend_theirs.1), channel_id=1, source_target_pairs={{0,2},{2,0},{4,6},{6,4},{8,10},{10,8},{12,14},{14,12},{16,18},{18,... | collective-permute-start | bytes 1671176 | tf_op jit(solution)/shard_map/ppermute | solution.py:465
  107.4 9.1 %copy-start = (f32[4,136,256]{2,1,0:T(8,128)S(1)}, f32[4,136,256]{2,1,0:T(8,128)}, u32[]{:S(2)}) copy-start(f32[4,136,256]{2,1,0:T(8,128)} %attend_mine.1.mine_ref) | copy-start | bytes 1671172
  117.4 23.5 %all-to-all-start.2 = ((bf16[16,192,128]{2,1,0:T(8,128)(2,1)}), bf16[16,192,128]{2,1,0:T(8,128)(2,1)S(1)}, u32[]{:S(2)}, u32[]{:S(2)}) async-start(bf16[16,192,128]{2,1,0:T(8,128)(2,1)} %join_shared.1), calls=%async_computation.2 | async-start | bytes 1572864 | tf_op jit(solution)/shard_map/all_to_all | solution.py:471
  148.0 7.2 %collective-permute-start.2 = (bf16[128,3072]{1,0:T(8,128)(2,1)S(1)}, bf16[128,3072]{1,0:T(8,128)(2,1)S(1)}, u32[]{:S(2)}, u32[]{:S(2)}) collective-permute-start(bf16[128,3072]{1,0:T(8,128)(2,1)S(1)} %project_theirs.1), channel_id=1, source_target_pairs={{0,1},{1,0},{2,3},{3,2},{4,5},{5,4},{6,7},{7,6},{8,9},{9,8},{10,11... | collective-permute-start | bytes 2359304 | tf_op jit(solution)/shard_map/ppermute | solution.py:478
  148.1 7.1 %copy-start.1 = (f32[3072]{0:T(1024)S(1)}, f32[3072]{0:T(1024)}, u32[]{:S(2)}) copy-start(f32[3072]{0:T(1024)} %param.17) | copy-start | bytes 36868
